TPU v7x, 32 devices: a whole 2x2x4 slice. The times are simulated.
32 devices in a mesh: rows: 16 (over z, y, x), cent: 2 (over core).
Axes of the slice: x: 2, y: 2, z: 4, core: 2. Of those that a mesh axis runs over, the one named last changes fastest.
Arguments:
- points: bfloat16 [16384, 1024], P('rows'), may hold values from -8 to 8
- centroids: bfloat16 [4096, 1024], P('cent'), may hold values from -8 to 8
- assign: int32 [16384], P('rows'), may hold values from 0 to 4095, as said below
Outputs:
- nearest: float32 [2, 16384], P(None, 'rows')
- updated: bfloat16 [4096, 1024], P('cent')
Inputs may be any that keep to these rules, and one draw needn't show every extreme that they name: `assign`: split the points into aligned blocks of 1024 and the centroids into aligned groups of 128 consecutive ones: in each block at most 64 points are assigned into any one group, and in every block some group takes exactly 64 of them.
All inputs are finite; a program needn't handle non-finite values.
Results may differ from a plain program's by a relative error of at most 0.001.
Values may be sent and summed in bfloat16 or wider, within the bound.
A program may use at most 64 MiB of HBM per device.

v0:
```python
import functools

import jax
import jax.numpy as jnp
from jax import lax
from jax.experimental import pallas as pl
from jax.experimental.pallas import tpu as pltpu
from jax.sharding import PartitionSpec as P


def smallest(points, pnorm, cents):
    cnorm = jnp.sum(jnp.square(cents.astype(jnp.float32)), axis=1)
    dots = lax.dot_general(
        points, cents, (((1,), (1,)), ((), ())), preferred_element_type=jnp.float32
    )
    return jnp.min((pnorm[:, None] - 2.0 * dots + cnorm[None, :]) / points.shape[1], axis=1)


def block_min(values):
    return lax.pmin(values, "cent")


def renew(part_sums, part_counts, own_rows):
    return ((part_sums + own_rows.astype(jnp.float32)) / (part_counts[:, None] + 1.0)).astype(
        jnp.bfloat16
    )


def per_device(points, centroids, assign):
    blocksize = centroids.shape[0]
    count_pts = points.shape[0]
    pnorm = jnp.sum(jnp.square(points.astype(jnp.float32)), axis=1)
    first = smallest(points, pnorm, centroids)
    first = block_min(first)
    relative = assign - lax.axis_index("cent") * blocksize
    share = blocksize // lax.axis_size("rows")
    own = lax.dynamic_slice_in_dim(centroids, lax.axis_index("rows") * share, share, 0)
    rows_count = lax.axis_size("rows")
    groups = rows_count * lax.axis_size("cent")
    capacity = max(2, 2 * count_pts // groups)
    inside = (relative >= 0) & (relative < blocksize)
    owners = jnp.where(inside, relative // share, rows_count)
    offsets = jnp.where(inside, relative - relative // share * share, 0)
    owner_hot = owners[:, None] == lax.broadcasted_iota(jnp.int32, (count_pts, rows_count), 1)
    earlier = lax.broadcasted_iota(jnp.int32, (count_pts, count_pts), 1) < lax.broadcasted_iota(
        jnp.int32, (count_pts, count_pts), 0
    )
    before = jnp.dot(
        earlier.astype(jnp.bfloat16),
        owner_hot.astype(jnp.bfloat16),
        preferred_element_type=jnp.float32,
    )
    ranking = jnp.sum(jnp.where(owner_hot, before, 0.0), axis=1).astype(jnp.int32)
    slot_index = jnp.where(inside, owners * capacity + ranking, -1)
    placing = (
        lax.broadcasted_iota(jnp.int32, (rows_count * capacity, count_pts), 0)
        == slot_index[None, :]
    )
    outgoing = jnp.dot(
        placing.astype(jnp.bfloat16), points, preferred_element_type=jnp.float32
    ).astype(jnp.bfloat16)
    labels = (jnp.sum(jnp.where(placing, offsets[None, :] + 1, 0), axis=1) - 1).astype(jnp.bfloat16)
    arrived, arrived_labels = (
        lax.all_to_all(outgoing, "rows", split_axis=0, concat_axis=0, tiled=True),
        lax.all_to_all(labels, "rows", split_axis=0, concat_axis=0, tiled=True),
    )
    chosen = (
        lax.broadcasted_iota(jnp.int32, (share, arrived.shape[0]), 0)
        == arrived_labels.astype(jnp.int32)[None, :]
    )
    part_sums = jnp.dot(chosen.astype(jnp.bfloat16), arrived, preferred_element_type=jnp.float32)
    part_counts = jnp.sum(chosen.astype(jnp.float32), axis=1)
    updated = lax.all_gather(renew(part_sums, part_counts, own), "rows", axis=0, tiled=True)
    second = smallest(points, pnorm, updated)
    nearest = jnp.stack([first, block_min(second)])
    return (nearest, updated)


PLANE = 4
LANES = 128
VMEM_BYTES = 53 * 1024 * 1024


def nt_dot(a, b):
    return lax.dot_general(a, b, (((1,), (1,)), ((), ())), preferred_element_type=jnp.float32)


def column_min(cents, points):
    wide = cents.astype(jnp.float32)
    cnorm = jnp.sum(wide * wide, axis=1, keepdims=True)
    return jnp.min(cnorm - 2.0 * nt_dot(cents, points), axis=0, keepdims=True)


def lloyd_kernel(
    rows, cap, share, assign_ref, points_hbm, cents_hbm, near_ref, upd_ref,
    points_ref, cents_ref, load_sem,
    send, lab_send, arrived, lab_arrived, acc, gath, mine, theirs, low,
    sent_pts, got_pts, sent_lab, got_lab, own_sem,
    sent_up, sent_down, sent_x, sent_y, got_full, sent_dx, sent_dy, got_dx, got_dy, out_sem, sent_min, got_min,
):
    count_pts, width = points_ref.shape
    blocksize = cents_ref.shape[0]
    planes = rows // PLANE
    per = LANES // cap
    me = lax.axis_index("rows")
    core = lax.axis_index("cent")
    z, q = me // PLANE, me % PLANE
    xpeer = me + 1 - 2 * (q % 2)
    ypeer = me + 2 - 4 * (q // 2)
    diag = ypeer + 1 - 2 * (q % 2)
    partner = 1 - core

    points_in = pltpu.make_async_copy(points_hbm, points_ref, load_sem.at[0])
    points_in.start()
    cents_in = pltpu.make_async_copy(cents_hbm, cents_ref, load_sem.at[1])
    cents_in.start()
    barrier = pltpu.get_barrier_semaphore()
    for step in range(1, rows):
        pl.semaphore_signal(barrier, inc=1, device_id={"rows": (me + step) % rows})
    pl.semaphore_signal(barrier, inc=1, device_id={"cent": partner})

    relative = (assign_ref[...] - core * blocksize).astype(jnp.float32)
    inside = (relative >= 0.0) & (relative < float(blocksize))
    owner = jnp.where(inside, jnp.floor(relative * (1.0 / share)), float(rows))
    offset1 = jnp.where(inside, relative - owner * share + 1.0, 0.0)
    hot = lax.broadcasted_iota(jnp.int32, (rows, count_pts), 0).astype(jnp.float32) == owner
    hot_f = jnp.where(hot, 1.0, 0.0)
    seg = 256
    tri = jnp.where(
        lax.broadcasted_iota(jnp.int32, (seg, seg), 0) < lax.broadcasted_iota(jnp.int32, (seg, seg), 1),
        1.0, 0.0,
    ).astype(jnp.bfloat16)
    carry = jnp.zeros((rows, 1), jnp.float32)
    pieces = []
    for s in range(count_pts // seg):
        part = hot_f[:, s * seg:(s + 1) * seg]
        before = jnp.dot(part.astype(jnp.bfloat16), tri, preferred_element_type=jnp.float32) + carry
        pieces.append(jnp.sum(part * before, axis=0, keepdims=True))
        carry = carry + jnp.sum(part, axis=1, keepdims=True)
    ranking = jnp.concatenate(pieces, axis=1)
    slot = jnp.where(inside, owner * cap + ranking, -1.0)
    labels8 = jnp.broadcast_to(offset1, (8, count_pts)).astype(jnp.bfloat16)

    points_in.wait()
    pl.semaphore_wait(barrier, rows)

    order = [planes // 2] + [o for o in range(1, planes) if o != planes // 2] + [0]
    chunk = PLANE * cap
    a2a = []

    def ship(src, dst, ss, rs, axis, target):
        copy = pltpu.make_async_remote_copy(
            src_ref=src, dst_ref=dst, send_sem=ss, recv_sem=rs, device_id={axis: target}
        )
        copy.start()
        return copy

    own_copies = []
    for j, o in enumerate(order):
        zt = (z + o) % planes
        placing = jnp.where(
            (lax.broadcasted_iota(jnp.int32, (chunk, count_pts), 0) + zt * chunk).astype(jnp.float32)
            == slot, 1.0, 0.0,
        ).astype(jnp.bfloat16)
        lab = nt_dot(labels8, placing)
        for t in range(chunk // LANES):
            lab_send[j, t] = lab[:, t * LANES:(t + 1) * LANES]
        send[j] = jnp.dot(
            placing, points_ref[...], preferred_element_type=jnp.float32
        ).astype(jnp.bfloat16)
        for k in range(PLANE):
            i = (q + k) % PLANE
            target = zt * PLANE + i
            piece = send.at[j, pl.ds(pl.multiple_of(i * cap, cap), cap)]
            lab_piece = lab_send.at[j, i // per]
            spot = arrived.at[me]
            if o == 0 and k == 0:
                for n, (a, b) in enumerate(((piece, spot), (lab_piece, lab_arrived.at[me]))):
                    c = pltpu.make_async_copy(a, b, own_sem.at[n])
                    c.start()
                    own_copies.append(c)
            else:
                n = j * PLANE + k
                a2a.append(ship(lab_piece, lab_arrived.at[me], sent_lab.at[n], got_lab.at[me], "rows", target))
                a2a.append(ship(piece, spot, sent_pts.at[n], got_pts.at[me], "rows", target))

    squares = jnp.square(points_ref[...].astype(jnp.float32))
    high = squares.astype(jnp.bfloat16)
    rest = (squares - high.astype(jnp.float32)).astype(jnp.bfloat16)
    ones = jnp.ones((8, width), jnp.bfloat16)
    pnorm = (nt_dot(ones, high) + nt_dot(ones, rest))[0:1, :]
    cents_in.wait()
    kb = 512
    low[...] = jnp.full(low.shape, jnp.inf, jnp.float32)

    def first_step(i, _):
        block = cents_ref[pl.ds(pl.multiple_of(i * kb, kb), kb), :]
        low[0:1, :] = jnp.minimum(low[0:1, :], column_min(block, points_ref[...]))
        return 0

    lax.fori_loop(0, blocksize // kb, first_step, 0)
    mine[0] = (pnorm + low[0:1, :]) / width
    min_copies = [ship(mine.at[0], theirs.at[0], sent_min.at[0], got_min.at[0], "cent", partner)]

    acc[...] = jnp.zeros_like(acc)
    counts = jnp.zeros((share, 1), jnp.float32)
    rowid1 = lax.broadcasted_iota(jnp.int32, (share, cap), 0).astype(jnp.float32) + 1.0
    for c in own_copies:
        c.wait()
    for o in [0] + [o for o in order if o != 0]:
        zs = (z + planes - o) % planes
        total = None
        for k in range(PLANE):
            i = (q + PLANE - k) % PLANE
            source = zs * PLANE + i
            if not (o == 0 and k == 0):
                for ref, sem in ((lab_arrived, got_lab), (arrived, got_pts)):
                    pltpu.make_async_remote_copy(
                        src_ref=ref.at[source], dst_ref=ref.at[source], send_sem=own_sem.at[0],
                        recv_sem=sem.at[source], device_id={"rows": source},
                    ).wait_recv()
            lab = lab_arrived[source]
            pick = lab[0:1, 0:cap]
            for t in range(1, per):
                pick = jnp.where(q % per == t, lab[0:1, t * cap:(t + 1) * cap], pick)
            chosen = jnp.where(rowid1 == pick, 1.0, 0.0)
            counts = counts + jnp.sum(chosen, axis=1, keepdims=True)
            acc[...] += jnp.dot(
                chosen.astype(jnp.bfloat16), arrived[source], preferred_element_type=jnp.float32
            )
    own_rows = cents_ref[pl.ds(pl.multiple_of(me * share, share), share), :]
    gath[me] = ((acc[...] + own_rows.astype(jnp.float32)) / (counts + 1.0)).astype(jnp.bfloat16)

    flying = []
    outs = []
    half = share // 2

    def pass_on(block, n):
        flying.append(ship(gath.at[block], gath.at[block], sent_x.at[n], got_full.at[block], "rows", xpeer))
        flying.append(ship(gath.at[block], gath.at[block], sent_y.at[n], got_full.at[block], "rows", ypeer))

    def await_full(block):
        pltpu.make_async_remote_copy(
            src_ref=gath.at[block], dst_ref=gath.at[block], send_sem=own_sem.at[0],
            recv_sem=got_full.at[block], device_id={"rows": xpeer},
        ).wait_recv()

    def await_part(block, part, sem):
        pltpu.make_async_remote_copy(
            src_ref=gath.at[block, part], dst_ref=gath.at[block, part], send_sem=own_sem.at[0],
            recv_sem=sem.at[block], device_id={"rows": xpeer},
        ).wait_recv()

    low[...] = jnp.full(low.shape, jnp.inf, jnp.float32)

    def absorb(block):
        c = pltpu.make_async_copy(gath.at[block], upd_ref.at[block], out_sem.at[block])
        c.start()
        outs.append(c)
        low[0:1, :] = jnp.minimum(low[0:1, :], column_min(gath[block], points_ref[...]))

    climbs = []

    def climb(block, n, upward, downward):
        for allowed, sems, toward in ((upward, sent_up, PLANE), (downward, sent_down, -PLANE)):
            @pl.when(allowed)
            def _(sems=sems, toward=toward):
                ship(gath.at[block], gath.at[block], sems.at[n], got_full.at[block], "rows", me + toward)
            climbs.append((block, n, allowed, sems, toward))

    upper, lower = pl.ds(0, half), pl.ds(half, half)
    top = z // 2
    visits = [z, z + 1 - 2 * (z % 2), 2 - top, 3 - 3 * top]
    climb(me, 0, z < planes - 1, z > 0)
    pass_on(me, 0)
    absorb(me)

    def cross(n):
        by, bx = visits[n] * PLANE + ypeer % PLANE, visits[n] * PLANE + xpeer % PLANE
        await_full(by)
        flying.append(ship(gath.at[by, upper], gath.at[by, upper], sent_dx.at[n], got_dx.at[by], "rows", xpeer))
        await_full(bx)
        flying.append(ship(gath.at[bx, lower], gath.at[bx, lower], sent_dy.at[n], got_dy.at[bx], "rows", ypeer))
        return by, bx

    for n in range(1, planes):
        zs = visits[n]
        block = zs * PLANE + q
        await_full(block)
        climb(block, n, (zs < z) & (z < planes - 1), (zs > z) & (z > 0))
        pass_on(block, n)
        ready = cross(n - 1)
        absorb(block)
        for b in ready:
            absorb(b)
    for b in cross(planes - 1):
        absorb(b)
    for zs in visits:
        bd = zs * PLANE + diag % PLANE
        await_part(bd, upper, got_dx)
        await_part(bd, lower, got_dy)
        absorb(bd)

    mine[1] = (pnorm + low[0:1, :]) / width
    min_copies.append(ship(mine.at[1], theirs.at[1], sent_min.at[1], got_min.at[1], "cent", partner))
    for copy in a2a + flying:
        copy.wait_send()
    for block, n, allowed, sems, toward in climbs:
        @pl.when(allowed)
        def _(block=block, n=n, sems=sems, toward=toward):
            pltpu.make_async_remote_copy(
                src_ref=gath.at[block], dst_ref=gath.at[block], send_sem=sems.at[n],
                recv_sem=got_full.at[block], device_id={"rows": me + toward},
            ).wait_send()
    for c in outs:
        c.wait()
    for n, copy in enumerate(min_copies):
        copy.wait()
        near_ref[n:n + 1, :] = jnp.minimum(mine[n], theirs[n])


def fused(points, centroids, assign, rows, cap, share):
    count_pts, width = points.shape
    planes = rows // PLANE
    hbm = pl.BlockSpec(memory_space=pltpu.HBM)
    vmem = pl.BlockSpec(memory_space=pltpu.VMEM)
    dma = pltpu.SemaphoreType.DMA
    chunk = PLANE * cap
    near, upd = pl.pallas_call(
        functools.partial(lloyd_kernel, rows, cap, share),
        out_shape=(
            jax.ShapeDtypeStruct((2, count_pts), jnp.float32),
            jax.ShapeDtypeStruct((rows, share, width), jnp.bfloat16),
        ),
        in_specs=[vmem, hbm, hbm],
        out_specs=(vmem, pl.BlockSpec(memory_space=pl.ANY)),
        scratch_shapes=[
            pltpu.VMEM((count_pts, width), jnp.bfloat16),
            pltpu.VMEM(centroids.shape, jnp.bfloat16),
            dma((2,)),
            pltpu.VMEM((planes, chunk, width), jnp.bfloat16),
            pltpu.VMEM((planes, chunk // LANES, 8, LANES), jnp.float32),
            pltpu.VMEM((rows, cap, width), jnp.bfloat16),
            pltpu.VMEM((rows, 8, LANES), jnp.float32),
            pltpu.VMEM((share, width), jnp.float32),
            pltpu.VMEM((rows, share, width), jnp.bfloat16),
            pltpu.VMEM((2, 1, count_pts), jnp.float32),
            pltpu.VMEM((2, 1, count_pts), jnp.float32),
            pltpu.VMEM((8, count_pts), jnp.float32),
            dma((rows,)), dma((rows,)), dma((rows,)), dma((rows,)), dma((2,)),
            dma((planes,)), dma((planes,)), dma((planes,)), dma((planes,)), dma((rows,)),
            dma((planes,)), dma((planes,)), dma((rows,)), dma((rows,)), dma((rows,)),
            dma((2,)), dma((2,)),
        ],
        compiler_params=pltpu.CompilerParams(
            collective_id=0, has_side_effects=True, vmem_limit_bytes=VMEM_BYTES
        ),
    )(assign[None, :], points, centroids)
    return near, upd.reshape(rows * share, width)


def step(rows, cent, points, centroids, assign):
    count_pts = points.shape[0]
    blocksize = centroids.shape[0]
    share = blocksize // rows
    cap = max(2, 2 * count_pts // (rows * cent))
    power = share & (share - 1) == 0 and cap & (cap - 1) == 0
    fits = cent == 2 and rows == 4 * PLANE and share % 32 == 0 and 16 <= cap <= LANES
    even = count_pts % 256 == 0 and blocksize % 512 == 0 and (PLANE * cap) % LANES == 0
    if power and fits and even:
        return fused(points, centroids, assign, rows, cap, share)
    return per_device(points, centroids, assign)


def solution(mesh):
    return jax.shard_map(
        functools.partial(step, mesh.shape["rows"], mesh.shape["cent"]),
        mesh=mesh,
        in_specs=(P("rows", None), P("cent", None), P("rows")),
        out_specs=(P(None, "rows"), P("cent", None)),
        check_vma=False,
    )
```

profile of v0, /device:TPU:0, one launch (start us, length us, event | category | flops | bytes accessed | tf_op | source)
XLA Modules:
  0.0 102.4 jit_solution(10186046285169960490)
XLA Ops:
  0.6 0.0 copy-start
  0.6 0.7 copy-done
  1.3 95.8 %shard_map.50 = (f32[2,1024]{1,0:T(2,128)S(1)}, bf16[16,128,1024]{2,1,0:T(8,128)(2,1)}) custom-call(s32[1,1024]{1,0:T(1,128)S(1)} %bitcast.2, bf16[1024,1024]{1,0:T(8,128)(2,1)} %points_hbm.1, bf16[2048,1024]{1,0:T(8,128)(2,1)} %cents_hbm.1), custom_call_target="tpu_custom_call" | custom-call | tf_op jit(solution)/shard_map/pallas_call | solution.py:329
  97.2 0.6 copy.7
  97.8 4.6 %copy.8 = bf16[2048,1024]{1,0:T(8,128)(2,1)} copy(bf16[2048,1024]{1,0:T(8,128)(2,1)} %bitcast.3) | data formatting | bytes 8388608
Async XLA Ops:
  0.6 0.7 copy-start
where the time goes:
time: 103 us; the launch traced here: 102 us
  Pallas kernels  95.8 us (93%)
  local copies, waits for them, and re-layouts  5.92 us (6%)
    pallas_call x1, Pallas kernels, fused(): pl.pallas_call(functools.partial(lloyd_kernel, rows, cap, share), out_sha...  95.8 us
    unnamed x4, local copies, waits for them, and re-layouts  5.92 us

commit v1 on v0

v1 whole, which is shorter than its diff:
```python
import functools

import jax
import jax.numpy as jnp
from jax import lax
from jax.experimental import pallas as pl
from jax.experimental.pallas import tpu as pltpu
from jax.sharding import PartitionSpec as P


def smallest(points, pnorm, cents):
    cnorm = jnp.sum(jnp.square(cents.astype(jnp.float32)), axis=1)
    dots = lax.dot_general(
        points, cents, (((1,), (1,)), ((), ())), preferred_element_type=jnp.float32
    )
    return jnp.min((pnorm[:, None] - 2.0 * dots + cnorm[None, :]) / points.shape[1], axis=1)


def block_min(values):
    return lax.pmin(values, "cent")


def renew(part_sums, part_counts, own_rows):
    return ((part_sums + own_rows.astype(jnp.float32)) / (part_counts[:, None] + 1.0)).astype(
        jnp.bfloat16
    )


def per_device(points, centroids, assign):
    blocksize = centroids.shape[0]
    count_pts = points.shape[0]
    pnorm = jnp.sum(jnp.square(points.astype(jnp.float32)), axis=1)
    first = smallest(points, pnorm, centroids)
    first = block_min(first)
    relative = assign - lax.axis_index("cent") * blocksize
    share = blocksize // lax.axis_size("rows")
    own = lax.dynamic_slice_in_dim(centroids, lax.axis_index("rows") * share, share, 0)
    rows_count = lax.axis_size("rows")
    groups = rows_count * lax.axis_size("cent")
    capacity = max(2, 2 * count_pts // groups)
    inside = (relative >= 0) & (relative < blocksize)
    owners = jnp.where(inside, relative // share, rows_count)
    offsets = jnp.where(inside, relative - relative // share * share, 0)
    owner_hot = owners[:, None] == lax.broadcasted_iota(jnp.int32, (count_pts, rows_count), 1)
    earlier = lax.broadcasted_iota(jnp.int32, (count_pts, count_pts), 1) < lax.broadcasted_iota(
        jnp.int32, (count_pts, count_pts), 0
    )
    before = jnp.dot(
        earlier.astype(jnp.bfloat16),
        owner_hot.astype(jnp.bfloat16),
        preferred_element_type=jnp.float32,
    )
    ranking = jnp.sum(jnp.where(owner_hot, before, 0.0), axis=1).astype(jnp.int32)
    slot_index = jnp.where(inside, owners * capacity + ranking, -1)
    placing = (
        lax.broadcasted_iota(jnp.int32, (rows_count * capacity, count_pts), 0)
        == slot_index[None, :]
    )
    outgoing = jnp.dot(
        placing.astype(jnp.bfloat16), points, preferred_element_type=jnp.float32
    ).astype(jnp.bfloat16)
    labels = (jnp.sum(jnp.where(placing, offsets[None, :] + 1, 0), axis=1) - 1).astype(jnp.bfloat16)
    arrived, arrived_labels = (
        lax.all_to_all(outgoing, "rows", split_axis=0, concat_axis=0, tiled=True),
        lax.all_to_all(labels, "rows", split_axis=0, concat_axis=0, tiled=True),
    )
    chosen = (
        lax.broadcasted_iota(jnp.int32, (share, arrived.shape[0]), 0)
        == arrived_labels.astype(jnp.int32)[None, :]
    )
    part_sums = jnp.dot(chosen.astype(jnp.bfloat16), arrived, preferred_element_type=jnp.float32)
    part_counts = jnp.sum(chosen.astype(jnp.float32), axis=1)
    updated = lax.all_gather(renew(part_sums, part_counts, own), "rows", axis=0, tiled=True)
    second = smallest(points, pnorm, updated)
    nearest = jnp.stack([first, block_min(second)])
    return (nearest, updated)


PLANE = 4
LANES = 128
VMEM_BYTES = 44 * 1024 * 1024
PARTS = 2


def nt_dot(a, b):
    return lax.dot_general(a, b, (((1,), (1,)), ((), ())), preferred_element_type=jnp.float32)


def column_min(cents, points):
    wide = cents.astype(jnp.float32)
    cnorm = jnp.sum(wide * wide, axis=1, keepdims=True)
    return jnp.min(cnorm - 2.0 * nt_dot(cents, points), axis=0, keepdims=True)


def flip(index, bits):
    low, high = index % 2, index // 2
    if bits % 2:
        low = 1 - low
    if bits // 2:
        high = 1 - high
    return high * 2 + low


def lloyd_kernel(
    rows, cap, share, assign_hbm, points_hbm, cents_hbm, near_ref, gath,
    assign_ref, points_ref, cents_ref, load_sem,
    placing_ref, send, lab_send, arrived, lab_arrived, klab,
    part_send, meta_send, part_got, meta_got, acc, mine, theirs, low,
    sent_pts, got_pts, sent_lab, got_lab, sent_part, got_part, sent_meta, got_meta,
    sent_up, sent_down, sent_x, sent_y, got_full, sent_dx, sent_dy, got_dx, got_dy, spare_sem, sent_min, got_min,
):
    count_pts, width = points_ref.shape
    blocksize = cents_ref.shape[0]
    planes = rows // PLANE
    wide = width // PARTS
    chunk = planes * cap
    me = lax.axis_index("rows")
    core = lax.axis_index("cent")
    z, q = me // PLANE, me % PLANE
    xpeer = z * PLANE + flip(q, 1)
    ypeer = z * PLANE + flip(q, 2)
    diag = z * PLANE + flip(q, 3)
    partner = 1 - core

    assign_in = pltpu.make_async_copy(assign_hbm, assign_ref, load_sem.at[2])
    assign_in.start()
    points_in = pltpu.make_async_copy(points_hbm, points_ref, load_sem.at[0])
    points_in.start()
    barrier = pltpu.get_barrier_semaphore()
    for bits in range(1, 4):
        pl.semaphore_signal(barrier, inc=1, device_id={"rows": z * PLANE + flip(q, bits)})
        pl.semaphore_signal(barrier, inc=1, device_id={"rows": flip(z, bits) * PLANE + q})
    pl.semaphore_signal(barrier, inc=1, device_id={"cent": partner})

    assign_in.wait()
    relative = (assign_ref[...] - core * blocksize).astype(jnp.float32)
    inside = (relative >= 0.0) & (relative < float(blocksize))
    owner = jnp.where(inside, jnp.floor(relative * (1.0 / share)), float(rows))
    offset1 = jnp.where(inside, relative - owner * share + 1.0, 0.0)
    hot = lax.broadcasted_iota(jnp.int32, (rows, count_pts), 0).astype(jnp.float32) == owner
    hot_f = jnp.where(hot, 1.0, 0.0)
    seg = 256
    tri = jnp.where(
        lax.broadcasted_iota(jnp.int32, (seg, seg), 0) < lax.broadcasted_iota(jnp.int32, (seg, seg), 1),
        1.0, 0.0,
    ).astype(jnp.bfloat16)
    carry = jnp.zeros((rows, 1), jnp.float32)
    pieces = []
    for s in range(count_pts // seg):
        part = hot_f[:, s * seg:(s + 1) * seg]
        before = jnp.dot(part.astype(jnp.bfloat16), tri, preferred_element_type=jnp.float32) + carry
        pieces.append(jnp.sum(part * before, axis=0, keepdims=True))
        carry = carry + jnp.sum(part, axis=1, keepdims=True)
    ranking = jnp.concatenate(pieces, axis=1)
    plane_to = jnp.floor(owner * (1.0 / PLANE))
    slot = jnp.where(inside, (owner - plane_to * PLANE) * chunk + plane_to * cap + ranking, -1.0)
    labels8 = jnp.broadcast_to(offset1, (8, count_pts)).astype(jnp.bfloat16)

    def ship(src, dst, ss, rs, axis, target):
        copy = pltpu.make_async_remote_copy(
            src_ref=src, dst_ref=dst, send_sem=ss, recv_sem=rs, device_id={axis: target}
        )
        copy.start()
        return copy

    def landed(ref, sem):
        pltpu.make_async_remote_copy(
            src_ref=ref, dst_ref=ref, send_sem=spare_sem.at[0], recv_sem=sem, device_id={"rows": xpeer}
        ).wait_recv()

    flying = []
    reach = (3, 1, 2)
    span = (2, 3, 1)

    def place(k):
        i = flip(q, k)
        hit = (
            lax.broadcasted_iota(jnp.int32, (chunk, count_pts), 0) + i * chunk
        ).astype(jnp.float32) == slot
        placing = jnp.where(hit, 1.0, 0.0).astype(jnp.bfloat16)
        placing_ref[k] = placing
        lab = nt_dot(labels8, placing)
        for t in range(chunk // LANES):
            piece = lab[:, t * LANES:(t + 1) * LANES]
            if k:
                lab_send[k, t] = piece
            else:
                lab_arrived[q, t] = piece

    def fill(h, k):
        rows_out = jnp.dot(
            placing_ref[k], points_ref[:, h * wide:(h + 1) * wide], preferred_element_type=jnp.float32
        ).astype(jnp.bfloat16)
        if k:
            send[h, k] = rows_out
        else:
            for t in range(planes):
                arrived[h, t, pl.ds(pl.multiple_of(q * cap, cap), cap), :] = rows_out[t * cap:(t + 1) * cap]

    def dispatch(h, j):
        t = flip(z, (span + (0,))[j])
        for k in reach:
            spot = pl.ds(pl.multiple_of(q * cap, cap), cap)
            flying.append(ship(
                send.at[h, k, pl.ds(pl.multiple_of(t * cap, cap), cap)], arrived.at[h, t, spot],
                sent_pts.at[h, j, k], got_pts.at[h, t, q], "rows", z * PLANE + flip(q, k),
            ))

    points_in.wait()
    cents_in = pltpu.make_async_copy(cents_hbm, cents_ref, load_sem.at[1])
    cents_in.start()
    for k in reach:
        place(k)
    for k in reach:
        fill(0, k)
    pl.semaphore_wait(barrier, 7)
    for k in reach:
        flying.append(ship(
            lab_send.at[k], lab_arrived.at[q], sent_lab.at[k], got_lab.at[q], "rows", z * PLANE + flip(q, k)
        ))
    for j in range(planes):
        dispatch(0, j)
    for h in range(1, PARTS):
        for k in reach:
            fill(h, k)
        for j in range(planes):
            dispatch(h, j)
    place(0)
    for h in range(PARTS):
        fill(h, 0)

    squares = jnp.square(points_ref[...].astype(jnp.float32))
    high = squares.astype(jnp.bfloat16)
    rest = (squares - high.astype(jnp.float32)).astype(jnp.bfloat16)
    ones = jnp.ones((8, width), jnp.bfloat16)
    pnorm = (nt_dot(ones, high) + nt_dot(ones, rest))[0:1, :]
    cents_in.wait()
    kb = 512
    low[...] = jnp.full(low.shape, jnp.inf, jnp.float32)

    def first_step(i, _):
        block = cents_ref[pl.ds(pl.multiple_of(i * kb, kb), kb), :]
        low[0:1, :] = jnp.minimum(low[0:1, :], column_min(block, points_ref[...]))
        return 0

    lax.fori_loop(0, blocksize // kb, first_step, 0)
    mine[0] = (pnorm + low[0:1, :]) / width
    min_copies = [ship(mine.at[0], theirs.at[0], sent_min.at[0], got_min.at[0], "cent", partner)]
    low[...] = jnp.full(low.shape, jnp.inf, jnp.float32)

    for k in reach:
        landed(lab_arrived.at[flip(q, k)], got_lab.at[flip(q, k)])
    lane = lax.broadcasted_iota(jnp.int32, (8, LANES), 1)
    for t in range(planes):
        for p in range(PLANE // 2):
            left, right = lab_arrived[2 * p, t // 2], lab_arrived[2 * p + 1, t // 2]
            if t % 2:
                left = pltpu.roll(left, cap, 1)
            else:
                right = pltpu.roll(right, cap, 1)
            klab[t, :, p * LANES:(p + 1) * LANES] = jnp.where(lane < cap, left, right)

    rowid1 = lax.broadcasted_iota(jnp.int32, (share, PLANE * cap), 0).astype(jnp.float32) + 1.0
    eye = lax.broadcasted_iota(jnp.int32, (share, LANES), 0) == lax.broadcasted_iota(
        jnp.int32, (share, LANES), 1
    )

    def to_row(column):
        return jnp.sum(jnp.where(eye, column, 0.0), axis=0, keepdims=True)

    def to_column(row):
        return jnp.sum(jnp.where(eye, row, 0.0), axis=1, keepdims=True)

    def gather_in(h, t):
        for k in reach:
            source = flip(q, k)
            landed(arrived.at[h, t, pl.ds(pl.multiple_of(source * cap, cap), cap)], got_pts.at[h, t, source])
        chosen = jnp.where(rowid1 == klab[t][0:1, :], 1.0, 0.0)
        counts = jnp.sum(chosen, axis=1, keepdims=True)
        total = jnp.dot(chosen.astype(jnp.bfloat16), arrived[h, t], preferred_element_type=jnp.float32)
        return total, counts

    def reduce_out(h):
        for j, bits in enumerate(span):
            t = flip(z, bits)
            total, counts = gather_in(h, t)
            peak = jnp.maximum(jnp.max(jnp.abs(total), axis=1, keepdims=True), 1e-30)
            grow = jnp.exp2(14.0 - jnp.floor(jnp.log2(peak)))
            grow = jnp.where(peak * grow >= 32767.0, grow * 0.5, grow)
            scaled = jnp.clip(jnp.round(total * grow), -32767.0, 32767.0)
            part_send[h, j] = scaled.astype(jnp.int32).astype(jnp.int16)
            first_row = lax.broadcasted_iota(jnp.int32, (8, LANES), 0) == 0
            meta_send[h, j] = jnp.where(first_row, to_row(1.0 / grow), to_row(counts))
            target = t * PLANE + q
            flying.append(ship(
                meta_send.at[h, j], meta_got.at[h, z], sent_meta.at[h, j], got_meta.at[h, z], "rows", target
            ))
            flying.append(ship(
                part_send.at[h, j], part_got.at[h, z], sent_part.at[h, j], got_part.at[h, z], "rows", target
            ))

    def renew_own(h):
        total, counts = gather_in(h, z)
        own_rows = cents_ref[pl.ds(pl.multiple_of(me * share, share), share), h * wide:(h + 1) * wide]
        acc[...] = total + own_rows.astype(jnp.float32)
        for bits in (1, 2, 3):
            t = flip(z, bits)
            landed(meta_got.at[h, t], got_meta.at[h, t])
            landed(part_got.at[h, t], got_part.at[h, t])
            meta = meta_got[h, t]
            counts = counts + to_column(meta[1:2, :])
            acc[...] += part_got[h, t].astype(jnp.int32).astype(jnp.float32) * to_column(meta[0:1, :])
        gath[me, :, h * wide:(h + 1) * wide] = (acc[...] / (counts + 1.0)).astype(jnp.bfloat16)

    half = share // 2
    upper, lower = pl.ds(0, half), pl.ds(half, half)
    top = z // 2
    visits = [z, z + 1 - 2 * (z % 2), 2 - top, 3 - 3 * top]
    climbs = []
    waiting = []

    def view(block, h, part=slice(None)):
        return gath.at[block, part, h * wide:(h + 1) * wide]

    def pass_on(h, block, n):
        for sem, target in ((sent_x, xpeer), (sent_y, ypeer)):
            flying.append(ship(view(block, h), view(block, h), sem.at[h, n], got_full.at[h, block], "rows", target))

    def climb(h, block, n, upward, downward):
        for allowed, sems, toward in ((upward, sent_up, PLANE), (downward, sent_down, -PLANE)):
            @pl.when(allowed)
            def _(sems=sems, toward=toward):
                ship(view(block, h), view(block, h), sems.at[h, n], got_full.at[h, block], "rows", me + toward)
            climbs.append((h, block, n, allowed, sems, toward))

    def await_full(h, block):
        landed(view(block, h), got_full.at[h, block])

    def absorb(h, *blocks):
        if h < PARTS - 1:
            return
        waiting.extend(blocks)
        while len(waiting) >= 2:
            drain(2)

    def drain(n):
        taken, waiting[:] = waiting[:n], waiting[n:]
        block = jnp.concatenate([gath[b] for b in taken], axis=0) if n > 1 else gath[taken[0]]
        low[0:1, :] = jnp.minimum(low[0:1, :], column_min(block, points_ref[...]))

    def cross(h, n):
        by, bx = visits[n] * PLANE + ypeer % PLANE, visits[n] * PLANE + xpeer % PLANE
        await_full(h, by)
        flying.append(ship(
            view(by, h, upper), view(by, h, upper), sent_dx.at[h, n], got_dx.at[h, by], "rows", xpeer
        ))
        await_full(h, bx)
        flying.append(ship(
            view(bx, h, lower), view(bx, h, lower), sent_dy.at[h, n], got_dy.at[h, bx], "rows", ypeer
        ))
        return by, bx

    def spread_start(h):
        climb(h, me, 0, z < planes - 1, z > 0)
        pass_on(h, me, 0)
        absorb(h, me)

    def spread_step(h, n):
        zs = visits[n]
        block = zs * PLANE + q
        await_full(h, block)
        climb(h, block, n, (zs < z) & (z < planes - 1), (zs > z) & (z > 0))
        pass_on(h, block, n)
        ready = cross(h, n - 1)
        absorb(h, block, *ready)

    def spread_end(h):
        absorb(h, *cross(h, planes - 1))

    def spread_rest(h):
        for zs in visits:
            bd = zs * PLANE + diag % PLANE
            landed(view(bd, h, upper), got_dx.at[h, bd])
            landed(view(bd, h, lower), got_dy.at[h, bd])
            absorb(h, bd)

    reduce_out(0)
    renew_own(0)
    spread_start(0)
    if PARTS == 1:
        for n in range(1, planes):
            spread_step(0, n)
        spread_end(0)
    else:
        reduce_out(1)
        spread_step(0, 1)
        renew_own(1)
        spread_start(1)
        spread_step(0, 2)
        spread_step(1, 1)
        spread_step(0, 3)
        spread_step(1, 2)
        spread_end(0)
        spread_step(1, 3)
        spread_rest(0)
        spread_end(1)
    spread_rest(PARTS - 1)
    if waiting:
        drain(len(waiting))

    mine[1] = (pnorm + low[0:1, :]) / width
    min_copies.append(ship(mine.at[1], theirs.at[1], sent_min.at[1], got_min.at[1], "cent", partner))
    for copy in flying:
        copy.wait_send()
    for h, block, n, allowed, sems, toward in climbs:
        @pl.when(allowed)
        def _(h=h, block=block, n=n, sems=sems, toward=toward):
            pltpu.make_async_remote_copy(
                src_ref=view(block, h), dst_ref=view(block, h), send_sem=sems.at[h, n],
                recv_sem=got_full.at[h, block], device_id={"rows": me + toward},
            ).wait_send()
    for n, copy in enumerate(min_copies):
        copy.wait()
        near_ref[n:n + 1, :] = jnp.minimum(mine[n], theirs[n])


def deliver(near_ref, gath_ref, near_out, upd_out, sems):
    copies = [
        pltpu.make_async_copy(gath_ref, upd_out, sems.at[0]),
        pltpu.make_async_copy(near_ref, near_out, sems.at[1]),
    ]
    for copy in copies:
        copy.start()
    for copy in copies:
        copy.wait()


def fused(points, centroids, assign, rows, cap, share):
    count_pts, width = points.shape
    planes = rows // PLANE
    hbm = pl.BlockSpec(memory_space=pltpu.HBM)
    vmem = pl.BlockSpec(memory_space=pltpu.VMEM)
    dma = pltpu.SemaphoreType.DMA
    chunk = planes * cap
    wide = width // PARTS
    shapes = (
        jax.ShapeDtypeStruct((2, count_pts), jnp.float32),
        jax.ShapeDtypeStruct((rows, share, width), jnp.bfloat16),
    )
    hops = planes - 1
    near, upd = pl.pallas_call(
        functools.partial(lloyd_kernel, rows, cap, share),
        out_shape=shapes,
        in_specs=[hbm, hbm, hbm],
        out_specs=(vmem, vmem),
        scratch_shapes=[
            pltpu.VMEM((1, count_pts), jnp.int32),
            pltpu.VMEM((count_pts, width), jnp.bfloat16),
            pltpu.VMEM(centroids.shape, jnp.bfloat16),
            dma((3,)),
            pltpu.VMEM((PLANE, chunk, count_pts), jnp.bfloat16),
            pltpu.VMEM((PARTS, PLANE, chunk, wide), jnp.bfloat16),
            pltpu.VMEM((PLANE, chunk // LANES, 8, LANES), jnp.float32),
            pltpu.VMEM((PARTS, planes, PLANE * cap, wide), jnp.bfloat16),
            pltpu.VMEM((PLANE, chunk // LANES, 8, LANES), jnp.float32),
            pltpu.VMEM((planes, 8, PLANE * cap), jnp.float32),
            pltpu.VMEM((PARTS, hops, share, wide), jnp.int16),
            pltpu.VMEM((PARTS, hops, 8, LANES), jnp.float32),
            pltpu.VMEM((PARTS, planes, share, wide), jnp.int16),
            pltpu.VMEM((PARTS, planes, 8, LANES), jnp.float32),
            pltpu.VMEM((share, wide), jnp.float32),
            pltpu.VMEM((2, 1, count_pts), jnp.float32),
            pltpu.VMEM((2, 1, count_pts), jnp.float32),
            pltpu.VMEM((8, count_pts), jnp.float32),
            dma((PARTS, planes, PLANE)), dma((PARTS, planes, PLANE)), dma((PLANE,)), dma((PLANE,)),
            dma((PARTS, hops)), dma((PARTS, planes)), dma((PARTS, hops)), dma((PARTS, planes)),
            dma((PARTS, planes)), dma((PARTS, planes)), dma((PARTS, planes)), dma((PARTS, planes)),
            dma((PARTS, rows)),
            dma((PARTS, planes)), dma((PARTS, planes)), dma((PARTS, rows)), dma((PARTS, rows)), dma((1,)),
            dma((2,)), dma((2,)),
        ],
        compiler_params=pltpu.CompilerParams(
            collective_id=0, has_side_effects=True, vmem_limit_bytes=VMEM_BYTES
        ),
    )(assign[None, :], points, centroids)
    near, upd = pl.pallas_call(
        deliver,
        out_shape=shapes,
        in_specs=[vmem, vmem],
        out_specs=(hbm, hbm),
        scratch_shapes=[dma((2,))],
    )(near, upd)
    return near, upd.reshape(rows * share, width)


def step(rows, cent, points, centroids, assign):
    count_pts = points.shape[0]
    blocksize = centroids.shape[0]
    share = blocksize // rows
    cap = max(2, 2 * count_pts // (rows * cent))
    fits = cent == 2 and rows == 4 * PLANE and share == LANES and 2 * cap == LANES
    even = count_pts % 256 == 0 and blocksize % 512 == 0 and points.shape[1] % (PARTS * LANES) == 0
    if fits and even:
        return fused(points, centroids, assign, rows, cap, share)
    return per_device(points, centroids, assign)


def solution(mesh):
    return jax.shard_map(
        functools.partial(step, mesh.shape["rows"], mesh.shape["cent"]),
        mesh=mesh,
        in_specs=(P("rows", None), P("cent", None), P("rows")),
        out_specs=(P(None, "rows"), P("cent", None)),
        check_vma=False,
    )
```

time: 103 us -> 90 us (0.87)
  Pallas kernels: 95.8 us -> 84.2 us
  local copies, waits for them, and re-layouts: 5.92 us -> 4.79 us
    pallas_call x1, Pallas kernels: 95.8 us -> 79.9 us  [fused(): pl.pallas_call(functools.partial(lloyd_kernel, rows, cap, share), out_sha...]
    pallas_call x0 -> x1, Pallas kernels: none -> 4.23 us  [fused(): pl.pallas_call(deliver, out_shape=shapes, in_specs=[vmem, vmem], out_spec...]
    unnamed x4 -> x8, local copies, waits for them, and re-layouts: 5.92 us -> 4.79 us
where the time goes in v1:
time: 90 us; the launch traced here: 89.8 us
  Pallas kernels  84.2 us (94%)
  local copies, waits for them, and re-layouts  4.79 us (5%)
    pallas_call x1, Pallas kernels, fused(): pl.pallas_call(functools.partial(lloyd_kernel, rows, cap, share), out_sha...  79.9 us
    unnamed x8, local copies, waits for them, and re-layouts  4.79 us
    pallas_call x1, Pallas kernels, fused(): pl.pallas_call(deliver, out_shape=shapes, in_specs=[vmem, vmem], out_spec...  4.23 us

profile of v1, /device:TPU:0, one launch (start us, length us, event | category | flops | bytes accessed | tf_op | source)
XLA Modules:
  0.0 89.8 jit_solution(11466858176133338138)
XLA Ops:
  0.6 0.0 copy-start.1
  0.6 1.6 %copy-done.1 = bf16[1024,1024]{1,0:T(8,128)(2,1)S(1)} copy-done((bf16[1024,1024]{1,0:T(8,128)(2,1)S(1)}, bf16[1024,1024]{1,0:T(8,128)(2,1)}, u32[]{:S(2)}) %copy-start.1) | copy-done | bytes 2097176
  2.2 0.0 copy-start.3
  2.2 0.7 copy-done.3
  2.9 79.9 %shard_map.50 = (f32[2,1024]{1,0:T(2,128)S(1)}, bf16[16,128,1024]{2,1,0:T(8,128)(2,1)S(1)}) custom-call(s32[1,1024]{1,0:T(1,128)S(1)} %bitcast.2, bf16[1024,1024]{1,0:T(8,128)(2,1)S(1)} %copy-done.1, bf16[2048,1024]{1,0:T(8,128)(2,1)} %cents_hbm.1), custom_call_target="tpu_custom_call" | custom-call | tf_op jit(solution)/shard_map/pallas_call | solution.py:451
  82.9 0.0 copy-start
  82.9 1.9 %copy-done = bf16[16,128,1024]{2,1,0:T(8,128)(2,1)} copy-done((bf16[16,128,1024]{2,1,0:T(8,128)(2,1)}, bf16[16,128,1024]{2,1,0:T(8,128)(2,1)S(1)}, u32[]{:S(2)}) %copy-start) | copy-done | bytes 4194328
  84.8 0.0 copy-start.2
  84.8 0.6 copy-done.2
  85.4 4.2 %shard_map.51 = (f32[2,1024]{1,0:T(2,128)}, bf16[16,128,1024]{2,1,0:T(8,128)(2,1)}) custom-call(f32[2,1024]{1,0:T(2,128)} %copy-done.2, bf16[16,128,1024]{2,1,0:T(8,128)(2,1)} %copy-done), custom_call_target="tpu_custom_call" | custom-call | tf_op jit(solution)/shard_map/pallas_call | solution.py:486
Async XLA Ops:
  0.6 1.6 %copy-start.1 = (bf16[1024,1024]{1,0:T(8,128)(2,1)S(1)}, bf16[1024,1024]{1,0:T(8,128)(2,1)}, u32[]{:S(2)}) copy-start(bf16[1024,1024]{1,0:T(8,128)(2,1)} %points_hbm.1) | copy-start | bytes 6291460
  2.2 0.7 copy-start.3
  82.9 1.9 %copy-start = (bf16[16,128,1024]{2,1,0:T(8,128)(2,1)}, bf16[16,128,1024]{2,1,0:T(8,128)(2,1)S(1)}, u32[]{:S(2)}) copy-start(bf16[16,128,1024]{2,1,0:T(8,128)(2,1)S(1)} %get-tuple-element.7.gath_ref) | copy-start | bytes 12582916
  84.8 0.6 copy-start.2

commit v2 on v1

--- a/solution.py
+++ b/solution.py
@@ -197,56 +197,54 @@
             for t in range(planes):
                 arrived[h, t, pl.ds(pl.multiple_of(q * cap, cap), cap), :] = rows_out[t * cap:(t + 1) * cap]
 
-    def dispatch(h, j):
+    def dispatch(h, j, k):
         t = flip(z, (span + (0,))[j])
-        for k in reach:
-            spot = pl.ds(pl.multiple_of(q * cap, cap), cap)
-            flying.append(ship(
-                send.at[h, k, pl.ds(pl.multiple_of(t * cap, cap), cap)], arrived.at[h, t, spot],
-                sent_pts.at[h, j, k], got_pts.at[h, t, q], "rows", z * PLANE + flip(q, k),
-            ))
+        spot = pl.ds(pl.multiple_of(q * cap, cap), cap)
+        flying.append(ship(
+            send.at[h, k, pl.ds(pl.multiple_of(t * cap, cap), cap)], arrived.at[h, t, spot],
+            sent_pts.at[h, j, k], got_pts.at[h, t, q], "rows", z * PLANE + flip(q, k),
+        ))
 
     points_in.wait()
     cents_in = pltpu.make_async_copy(cents_hbm, cents_ref, load_sem.at[1])
     cents_in.start()
     for k in reach:
         place(k)
-    for k in reach:
         fill(0, k)
-    pl.semaphore_wait(barrier, 7)
-    for k in reach:
+        if k == reach[0]:
+            pl.semaphore_wait(barrier, 7)
         flying.append(ship(
             lab_send.at[k], lab_arrived.at[q], sent_lab.at[k], got_lab.at[q], "rows", z * PLANE + flip(q, k)
         ))
-    for j in range(planes):
-        dispatch(0, j)
+        for j in range(planes // 2):
+            dispatch(0, j, k)
+    for j in range(planes // 2, planes):
+        for k in reach:
+            dispatch(0, j, k)
     for h in range(1, PARTS):
         for k in reach:
             fill(h, k)
         for j in range(planes):
-            dispatch(h, j)
+            for k in reach:
+                dispatch(h, j, k)
     place(0)
     for h in range(PARTS):
         fill(h, 0)
 
-    squares = jnp.square(points_ref[...].astype(jnp.float32))
-    high = squares.astype(jnp.bfloat16)
-    rest = (squares - high.astype(jnp.float32)).astype(jnp.bfloat16)
-    ones = jnp.ones((8, width), jnp.bfloat16)
-    pnorm = (nt_dot(ones, high) + nt_dot(ones, rest))[0:1, :]
-    cents_in.wait()
     kb = 512
+    pieces_first = blocksize // kb
     low[...] = jnp.full(low.shape, jnp.inf, jnp.float32)
-
-    def first_step(i, _):
-        block = cents_ref[pl.ds(pl.multiple_of(i * kb, kb), kb), :]
-        low[0:1, :] = jnp.minimum(low[0:1, :], column_min(block, points_ref[...]))
-        return 0
-
-    lax.fori_loop(0, blocksize // kb, first_step, 0)
-    mine[0] = (pnorm + low[0:1, :]) / width
-    min_copies = [ship(mine.at[0], theirs.at[0], sent_min.at[0], got_min.at[0], "cent", partner)]
-    low[...] = jnp.full(low.shape, jnp.inf, jnp.float32)
+    min_copies = []
+
+    def first_piece(i):
+        low[0:1, :] = jnp.minimum(low[0:1, :], column_min(cents_ref[i * kb:(i + 1) * kb, :], points_ref[...]))
+
+    def point_norms():
+        squares = jnp.square(points_ref[...].astype(jnp.float32))
+        high = squares.astype(jnp.bfloat16)
+        rest = (squares - high.astype(jnp.float32)).astype(jnp.bfloat16)
+        ones = jnp.ones((8, width), jnp.bfloat16)
+        return (nt_dot(ones, high) + nt_dot(ones, rest))[0:1, :]
 
     for k in reach:
         landed(lab_arrived.at[flip(q, k)], got_lab.at[flip(q, k)])
@@ -280,37 +278,39 @@
         total = jnp.dot(chosen.astype(jnp.bfloat16), arrived[h, t], preferred_element_type=jnp.float32)
         return total, counts
 
-    def reduce_out(h):
-        for j, bits in enumerate(span):
-            t = flip(z, bits)
-            total, counts = gather_in(h, t)
-            peak = jnp.maximum(jnp.max(jnp.abs(total), axis=1, keepdims=True), 1e-30)
-            grow = jnp.exp2(14.0 - jnp.floor(jnp.log2(peak)))
-            grow = jnp.where(peak * grow >= 32767.0, grow * 0.5, grow)
-            scaled = jnp.clip(jnp.round(total * grow), -32767.0, 32767.0)
-            part_send[h, j] = scaled.astype(jnp.int32).astype(jnp.int16)
-            first_row = lax.broadcasted_iota(jnp.int32, (8, LANES), 0) == 0
-            meta_send[h, j] = jnp.where(first_row, to_row(1.0 / grow), to_row(counts))
-            target = t * PLANE + q
-            flying.append(ship(
-                meta_send.at[h, j], meta_got.at[h, z], sent_meta.at[h, j], got_meta.at[h, z], "rows", target
-            ))
-            flying.append(ship(
-                part_send.at[h, j], part_got.at[h, z], sent_part.at[h, j], got_part.at[h, z], "rows", target
-            ))
-
-    def renew_own(h):
+    def reduce_out(h, j):
+        t = flip(z, span[j])
+        total, counts = gather_in(h, t)
+        peak = jnp.maximum(jnp.max(jnp.abs(total), axis=1, keepdims=True), 1e-30)
+        grow = jnp.exp2(14.0 - jnp.floor(jnp.log2(peak)))
+        grow = jnp.where(peak * grow >= 32767.0, grow * 0.5, grow)
+        scaled = jnp.clip(jnp.round(total * grow), -32767.0, 32767.0)
+        part_send[h, j] = scaled.astype(jnp.int32).astype(jnp.int16)
+        first_row = lax.broadcasted_iota(jnp.int32, (8, LANES), 0) == 0
+        meta_send[h, j] = jnp.where(first_row, to_row(1.0 / grow), to_row(counts))
+        target = t * PLANE + q
+        flying.append(ship(
+            meta_send.at[h, j], meta_got.at[h, z], sent_meta.at[h, j], got_meta.at[h, z], "rows", target
+        ))
+        flying.append(ship(
+            part_send.at[h, j], part_got.at[h, z], sent_part.at[h, j], got_part.at[h, z], "rows", target
+        ))
+
+    def reduce_own(h):
         total, counts = gather_in(h, z)
         own_rows = cents_ref[pl.ds(pl.multiple_of(me * share, share), share), h * wide:(h + 1) * wide]
-        acc[...] = total + own_rows.astype(jnp.float32)
+        acc[h] = total + own_rows.astype(jnp.float32)
+        return counts
+
+    def renew_own(h, counts):
         for bits in (1, 2, 3):
             t = flip(z, bits)
             landed(meta_got.at[h, t], got_meta.at[h, t])
             landed(part_got.at[h, t], got_part.at[h, t])
             meta = meta_got[h, t]
             counts = counts + to_column(meta[1:2, :])
-            acc[...] += part_got[h, t].astype(jnp.int32).astype(jnp.float32) * to_column(meta[0:1, :])
-        gath[me, :, h * wide:(h + 1) * wide] = (acc[...] / (counts + 1.0)).astype(jnp.bfloat16)
+            acc[h] += part_got[h, t].astype(jnp.int32).astype(jnp.float32) * to_column(meta[0:1, :])
+        gath[me, :, h * wide:(h + 1) * wide] = (acc[h] / (counts + 1.0)).astype(jnp.bfloat16)
 
     half = share // 2
     upper, lower = pl.ds(0, half), pl.ds(half, half)
@@ -346,7 +346,7 @@
     def drain(n):
         taken, waiting[:] = waiting[:n], waiting[n:]
         block = jnp.concatenate([gath[b] for b in taken], axis=0) if n > 1 else gath[taken[0]]
-        low[0:1, :] = jnp.minimum(low[0:1, :], column_min(block, points_ref[...]))
+        low[1:2, :] = jnp.minimum(low[1:2, :], column_min(block, points_ref[...]))
 
     def cross(h, n):
         by, bx = visits[n] * PLANE + ypeer % PLANE, visits[n] * PLANE + xpeer % PLANE
@@ -384,31 +384,38 @@
             landed(view(bd, h, lower), got_dy.at[h, bd])
             absorb(h, bd)
 
-    reduce_out(0)
-    renew_own(0)
+    cents_in.wait()
+    for j in range(planes - 1):
+        reduce_out(0, j)
+        first_piece(j)
+    counts = reduce_own(0)
+    for i in range(planes - 1, pieces_first):
+        first_piece(i)
+    reduce_out(1, 0)
+    renew_own(0, counts)
     spread_start(0)
-    if PARTS == 1:
-        for n in range(1, planes):
-            spread_step(0, n)
-        spread_end(0)
-    else:
-        reduce_out(1)
-        spread_step(0, 1)
-        renew_own(1)
-        spread_start(1)
-        spread_step(0, 2)
-        spread_step(1, 1)
-        spread_step(0, 3)
-        spread_step(1, 2)
-        spread_end(0)
-        spread_step(1, 3)
-        spread_rest(0)
-        spread_end(1)
-    spread_rest(PARTS - 1)
+    reduce_out(1, 1)
+    pnorm = point_norms()
+    mine[0] = (pnorm + low[0:1, :]) / width
+    min_copies.append(ship(mine.at[0], theirs.at[0], sent_min.at[0], got_min.at[0], "cent", partner))
+    reduce_out(1, 2)
+    spread_step(0, 1)
+    counts = reduce_own(1)
+    renew_own(1, counts)
+    spread_start(1)
+    spread_step(0, 2)
+    spread_step(1, 1)
+    spread_step(0, 3)
+    spread_step(1, 2)
+    spread_end(0)
+    spread_step(1, 3)
+    spread_rest(0)
+    spread_end(1)
+    spread_rest(1)
     if waiting:
         drain(len(waiting))
 
-    mine[1] = (pnorm + low[0:1, :]) / width
+    mine[1] = (pnorm + low[1:2, :]) / width
     min_copies.append(ship(mine.at[1], theirs.at[1], sent_min.at[1], got_min.at[1], "cent", partner))
     for copy in flying:
         copy.wait_send()
@@ -468,7 +475,7 @@
             pltpu.VMEM((PARTS, hops, 8, LANES), jnp.float32),
             pltpu.VMEM((PARTS, planes, share, wide), jnp.int16),
             pltpu.VMEM((PARTS, planes, 8, LANES), jnp.float32),
-            pltpu.VMEM((share, wide), jnp.float32),
+            pltpu.VMEM((PARTS, share, wide), jnp.float32),
             pltpu.VMEM((2, 1, count_pts), jnp.float32),
             pltpu.VMEM((2, 1, count_pts), jnp.float32),
             pltpu.VMEM((8, count_pts), jnp.float32),
@@ -482,13 +489,18 @@
         compiler_params=pltpu.CompilerParams(
             collective_id=0, has_side_effects=True, vmem_limit_bytes=VMEM_BYTES
         ),
-    )(assign[None, :], points, centroids)
+    )(
+        pltpu.with_memory_space_constraint(assign[None, :], pltpu.HBM),
+        pltpu.with_memory_space_constraint(points, pltpu.HBM),
+        pltpu.with_memory_space_constraint(centroids, pltpu.HBM),
+    )
     near, upd = pl.pallas_call(
         deliver,
         out_shape=shapes,
         in_specs=[vmem, vmem],
         out_specs=(hbm, hbm),
         scratch_shapes=[dma((2,))],
+        compiler_params=pltpu.CompilerParams(vmem_limit_bytes=1024 * 1024),
     )(near, upd)
     return near, upd.reshape(rows * share, width)
 

time: 90 us -> 80.5 us (0.89)
  local copies, waits for them, and re-layouts: 4.79 us -> 0 us
  Pallas kernels: 84.2 us -> 79.5 us
    unnamed x8 -> x0, local copies, waits for them, and re-layouts: 4.79 us -> none
    pallas_call x1, Pallas kernels: 79.9 us -> 77.5 us  [fused(): pl.pallas_call(functools.partial(lloyd_kernel, rows, cap, share), out_sha...]
    pallas_call x1, Pallas kernels: 4.23 us -> 2.03 us  [fused(): pl.pallas_call(deliver, out_shape=shapes, in_specs=[vmem, vmem], out_spec...]
where the time goes in v2:
time: 80.5 us; the launch traced here: 80.3 us
  Pallas kernels  79.5 us (99%)
    pallas_call x1, Pallas kernels, fused(): pl.pallas_call(functools.partial(lloyd_kernel, rows, cap, share), out_sha...  77.5 us
    pallas_call x1, Pallas kernels, fused(): pl.pallas_call(deliver, out_shape=shapes, in_specs=[vmem, vmem], out_spec...  2.03 us

profile of v2, /device:TPU:0, one launch (start us, length us, event | category | flops | bytes accessed | tf_op | source)
XLA Modules:
  0.0 80.3 jit_solution(6747648507898216434)
XLA Ops:
  0.6 77.5 %shard_map.50 = (f32[2,1024]{1,0:T(2,128)S(1)}, bf16[16,128,1024]{2,1,0:T(8,128)(2,1)S(1)}) custom-call(s32[1,1024]{1,0:T(1,128)} %bitcast.2, bf16[1024,1024]{1,0:T(8,128)(2,1)} %points_hbm.1, bf16[2048,1024]{1,0:T(8,128)(2,1)} %cents_hbm.1), custom_call_target="tpu_custom_call" | custom-call | tf_op jit(solution)/shard_map/pallas_call | solution.py:458
  78.1 2.0 %shard_map.51 = (f32[2,1024]{1,0:T(2,128)}, bf16[16,128,1024]{2,1,0:T(8,128)(2,1)}) custom-call(f32[2,1024]{1,0:T(2,128)S(1)} %get-tuple-element.6.near_ref, bf16[16,128,1024]{2,1,0:T(8,128)(2,1)S(1)} %get-tuple-element.7.gath_ref), custom_call_target="tpu_custom_call" | custom-call | tf_op jit(solution)/shard_map/pallas_call | solution.py:497

commit v3 on v2

--- a/solution.py
+++ b/solution.py
@@ -105,7 +105,7 @@
     rows, cap, share, assign_hbm, points_hbm, cents_hbm, near_ref, gath,
     assign_ref, points_ref, cents_ref, load_sem,
     placing_ref, send, lab_send, arrived, lab_arrived, klab,
-    part_send, meta_send, part_got, meta_got, acc, mine, theirs, low,
+    part_send, meta_send, part_got, meta_got, acc, held, mine, theirs, low,
     sent_pts, got_pts, sent_lab, got_lab, sent_part, got_part, sent_meta, got_meta,
     sent_up, sent_down, sent_x, sent_y, got_full, sent_dx, sent_dy, got_dx, got_dy, spare_sem, sent_min, got_min,
 ):
@@ -170,7 +170,7 @@
 
     flying = []
     reach = (3, 1, 2)
-    span = (2, 3, 1)
+    span = (3, 2, 1, 0)
 
     def place(k):
         i = flip(q, k)
@@ -198,7 +198,7 @@
                 arrived[h, t, pl.ds(pl.multiple_of(q * cap, cap), cap), :] = rows_out[t * cap:(t + 1) * cap]
 
     def dispatch(h, j, k):
-        t = flip(z, (span + (0,))[j])
+        t = flip(z, span[j])
         spot = pl.ds(pl.multiple_of(q * cap, cap), cap)
         flying.append(ship(
             send.at[h, k, pl.ds(pl.multiple_of(t * cap, cap), cap)], arrived.at[h, t, spot],
@@ -216,9 +216,8 @@
         flying.append(ship(
             lab_send.at[k], lab_arrived.at[q], sent_lab.at[k], got_lab.at[q], "rows", z * PLANE + flip(q, k)
         ))
-        for j in range(planes // 2):
-            dispatch(0, j, k)
-    for j in range(planes // 2, planes):
+        dispatch(0, 0, k)
+    for j in range(1, planes):
         for k in reach:
             dispatch(0, j, k)
     for h in range(1, PARTS):
@@ -278,23 +277,43 @@
         total = jnp.dot(chosen.astype(jnp.bfloat16), arrived[h, t], preferred_element_type=jnp.float32)
         return total, counts
 
-    def reduce_out(h, j):
-        t = flip(z, span[j])
-        total, counts = gather_in(h, t)
+    def send_part(h, n, total, counts, target):
         peak = jnp.maximum(jnp.max(jnp.abs(total), axis=1, keepdims=True), 1e-30)
         grow = jnp.exp2(14.0 - jnp.floor(jnp.log2(peak)))
         grow = jnp.where(peak * grow >= 32767.0, grow * 0.5, grow)
         scaled = jnp.clip(jnp.round(total * grow), -32767.0, 32767.0)
-        part_send[h, j] = scaled.astype(jnp.int32).astype(jnp.int16)
+        part_send[h, n] = scaled.astype(jnp.int32).astype(jnp.int16)
         first_row = lax.broadcasted_iota(jnp.int32, (8, LANES), 0) == 0
-        meta_send[h, j] = jnp.where(first_row, to_row(1.0 / grow), to_row(counts))
-        target = t * PLANE + q
+        meta_send[h, n] = jnp.where(first_row, to_row(1.0 / grow), to_row(counts))
         flying.append(ship(
-            meta_send.at[h, j], meta_got.at[h, z], sent_meta.at[h, j], got_meta.at[h, z], "rows", target
+            meta_send.at[h, n], meta_got.at[h, n], sent_meta.at[h, n], got_meta.at[h, n], "rows", target
         ))
         flying.append(ship(
-            part_send.at[h, j], part_got.at[h, z], sent_part.at[h, j], got_part.at[h, z], "rows", target
+            part_send.at[h, n], part_got.at[h, n], sent_part.at[h, n], got_part.at[h, n], "rows", target
         ))
+
+    def take_part(h, n):
+        landed(meta_got.at[h, n], got_meta.at[h, n])
+        landed(part_got.at[h, n], got_part.at[h, n])
+        meta = meta_got[h, n]
+        return part_got[h, n].astype(jnp.int32).astype(jnp.float32) * to_column(meta[0:1, :]), to_column(meta[1:2, :])
+
+    near_plane, far_plane = flip(z, 1) * PLANE + q, flip(z, 2) * PLANE + q
+
+    def reduce_cross(h):
+        send_part(h, 0, *gather_in(h, flip(z, 3)), near_plane)
+
+    def reduce_hold(h):
+        total, counts = gather_in(h, flip(z, 2))
+        held[h] = total
+        return counts
+
+    def reduce_far(h, counts):
+        more, extra = take_part(h, 0)
+        send_part(h, 1, held[h] + more, counts + extra, far_plane)
+
+    def reduce_near(h):
+        send_part(h, 2, *gather_in(h, flip(z, 1)), near_plane)
 
     def reduce_own(h):
         total, counts = gather_in(h, z)
@@ -303,14 +322,11 @@
         return counts
 
     def renew_own(h, counts):
-        for bits in (1, 2, 3):
-            t = flip(z, bits)
-            landed(meta_got.at[h, t], got_meta.at[h, t])
-            landed(part_got.at[h, t], got_part.at[h, t])
-            meta = meta_got[h, t]
-            counts = counts + to_column(meta[1:2, :])
-            acc[h] += part_got[h, t].astype(jnp.int32).astype(jnp.float32) * to_column(meta[0:1, :])
-        gath[me, :, h * wide:(h + 1) * wide] = (acc[h] / (counts + 1.0)).astype(jnp.bfloat16)
+        total = acc[h]
+        for n in (2, 1):
+            more, extra = take_part(h, n)
+            total, counts = total + more, counts + extra
+        gath[me, :, h * wide:(h + 1) * wide] = (total / (counts + 1.0)).astype(jnp.bfloat16)
 
     half = share // 2
     upper, lower = pl.ds(0, half), pl.ds(half, half)
@@ -371,11 +387,10 @@
         await_full(h, block)
         climb(h, block, n, (zs < z) & (z < planes - 1), (zs > z) & (z > 0))
         pass_on(h, block, n)
-        ready = cross(h, n - 1)
-        absorb(h, block, *ready)
-
-    def spread_end(h):
-        absorb(h, *cross(h, planes - 1))
+        absorb(h, block)
+
+    def spread_cross(h, n):
+        absorb(h, *cross(h, n))
 
     def spread_rest(h):
         for zs in visits:
@@ -385,32 +400,43 @@
             absorb(h, bd)
 
     cents_in.wait()
-    for j in range(planes - 1):
-        reduce_out(0, j)
-        first_piece(j)
+    reduce_cross(0)
+    first_piece(0)
+    counts = reduce_hold(0)
+    first_piece(1)
+    reduce_far(0, counts)
+    reduce_near(0)
+    first_piece(2)
     counts = reduce_own(0)
     for i in range(planes - 1, pieces_first):
         first_piece(i)
-    reduce_out(1, 0)
     renew_own(0, counts)
     spread_start(0)
-    reduce_out(1, 1)
+    reduce_cross(1)
     pnorm = point_norms()
     mine[0] = (pnorm + low[0:1, :]) / width
     min_copies.append(ship(mine.at[0], theirs.at[0], sent_min.at[0], got_min.at[0], "cent", partner))
-    reduce_out(1, 2)
+    counts = reduce_hold(1)
+    reduce_far(1, counts)
+    reduce_near(1)
     spread_step(0, 1)
     counts = reduce_own(1)
     renew_own(1, counts)
     spread_start(1)
     spread_step(0, 2)
+    spread_cross(0, 0)
     spread_step(1, 1)
     spread_step(0, 3)
+    spread_cross(0, 1)
     spread_step(1, 2)
-    spread_end(0)
+    spread_cross(1, 0)
+    spread_cross(0, 2)
     spread_step(1, 3)
+    spread_cross(1, 1)
+    spread_cross(0, 3)
+    spread_cross(1, 2)
     spread_rest(0)
-    spread_end(1)
+    spread_cross(1, 3)
     spread_rest(1)
     if waiting:
         drain(len(waiting))
@@ -473,14 +499,15 @@
             pltpu.VMEM((planes, 8, PLANE * cap), jnp.float32),
             pltpu.VMEM((PARTS, hops, share, wide), jnp.int16),
             pltpu.VMEM((PARTS, hops, 8, LANES), jnp.float32),
-            pltpu.VMEM((PARTS, planes, share, wide), jnp.int16),
-            pltpu.VMEM((PARTS, planes, 8, LANES), jnp.float32),
+            pltpu.VMEM((PARTS, hops, share, wide), jnp.int16),
+            pltpu.VMEM((PARTS, hops, 8, LANES), jnp.float32),
+            pltpu.VMEM((PARTS, share, wide), jnp.float32),
             pltpu.VMEM((PARTS, share, wide), jnp.float32),
             pltpu.VMEM((2, 1, count_pts), jnp.float32),
             pltpu.VMEM((2, 1, count_pts), jnp.float32),
             pltpu.VMEM((8, count_pts), jnp.float32),
             dma((PARTS, planes, PLANE)), dma((PARTS, planes, PLANE)), dma((PLANE,)), dma((PLANE,)),
-            dma((PARTS, hops)), dma((PARTS, planes)), dma((PARTS, hops)), dma((PARTS, planes)),
+            dma((PARTS, hops)), dma((PARTS, hops)), dma((PARTS, hops)), dma((PARTS, hops)),
             dma((PARTS, planes)), dma((PARTS, planes)), dma((PARTS, planes)), dma((PARTS, planes)),
             dma((PARTS, rows)),
             dma((PARTS, planes)), dma((PARTS, planes)), dma((PARTS, rows)), dma((PARTS, rows)), dma((1,)),

time: 80.5 us -> 78.8 us (0.979)
  Pallas kernels: 79.5 us -> 77.8 us
    pallas_call x1, Pallas kernels: 77.5 us -> 75.8 us  [fused(): pl.pallas_call(functools.partial(lloyd_kernel, rows, cap, share), out_sha...]
where the time goes in v3:
time: 78.8 us; the launch traced here: 78.6 us
  Pallas kernels  77.8 us (99%)
  between operations  0.8 us (1%)
    pallas_call x1, Pallas kernels, fused(): pl.pallas_call(functools.partial(lloyd_kernel, rows, cap, share), out_sha...  75.8 us
    pallas_call x1, Pallas kernels, fused(): pl.pallas_call(deliver, out_shape=shapes, in_specs=[vmem, vmem], out_spec...  2.03 us

profile of v3, /device:TPU:0, one launch (start us, length us, event | category | flops | bytes accessed | tf_op | source)
XLA Modules:
  0.0 78.6 jit_solution(9850043515588644634)
XLA Ops:
  0.6 75.8 %shard_map.50 = (f32[2,1024]{1,0:T(2,128)S(1)}, bf16[16,128,1024]{2,1,0:T(8,128)(2,1)S(1)}) custom-call(s32[1,1024]{1,0:T(1,128)} %bitcast.2, bf16[1024,1024]{1,0:T(8,128)(2,1)} %points_hbm.1, bf16[2048,1024]{1,0:T(8,128)(2,1)} %cents_hbm.1), custom_call_target="tpu_custom_call" | custom-call | tf_op jit(solution)/shard_map/pallas_call | solution.py:484
  76.4 2.0 %shard_map.51 = (f32[2,1024]{1,0:T(2,128)}, bf16[16,128,1024]{2,1,0:T(8,128)(2,1)}) custom-call(f32[2,1024]{1,0:T(2,128)S(1)} %get-tuple-element.6.near_ref, bf16[16,128,1024]{2,1,0:T(8,128)(2,1)S(1)} %get-tuple-element.7.gath_ref), custom_call_target="tpu_custom_call" | custom-call | tf_op jit(solution)/shard_map/pallas_call | solution.py:524

commit v4 on v3

--- a/solution.py
+++ b/solution.py
@@ -80,6 +80,7 @@
 LANES = 128
 VMEM_BYTES = 44 * 1024 * 1024
 PARTS = 2
+TALL = (0, 64)
 
 
 def nt_dot(a, b):
@@ -107,7 +108,7 @@
     placing_ref, send, lab_send, arrived, lab_arrived, klab,
     part_send, meta_send, part_got, meta_got, acc, held, mine, theirs, low,
     sent_pts, got_pts, sent_lab, got_lab, sent_part, got_part, sent_meta, got_meta,
-    sent_up, sent_down, sent_x, sent_y, got_full, sent_dx, sent_dy, got_dx, got_dy, spare_sem, sent_min, got_min,
+    sent_up, sent_down, got_col, sent_up_tall, sent_down_tall, got_tall, sent_x, sent_y, got_full, sent_dx, sent_dy, got_dx, got_dy, spare_sem, sent_min, got_min,
 ):
     count_pts, width = points_ref.shape
     blocksize = cents_ref.shape[0]
@@ -328,34 +329,41 @@
             total, counts = total + more, counts + extra
         gath[me, :, h * wide:(h + 1) * wide] = (total / (counts + 1.0)).astype(jnp.bfloat16)
 
-    half = share // 2
-    upper, lower = pl.ds(0, half), pl.ds(half, half)
     top = z // 2
     visits = [z, z + 1 - 2 * (z % 2), 2 - top, 3 - 3 * top]
     climbs = []
     waiting = []
-
-    def view(block, h, part=slice(None)):
-        return gath.at[block, part, h * wide:(h + 1) * wide]
+    missing = {}
+
+    def flat(h, n):
+        return share if n == 0 else share - TALL[h]
+
+    def view(block, h, first=0, count=share):
+        return gath.at[block, pl.ds(first, count), h * wide:(h + 1) * wide]
+
+    def tall(block, h):
+        return view(block, h, share - TALL[h], TALL[h])
 
     def pass_on(h, block, n):
+        part = view(block, h, 0, flat(h, n))
         for sem, target in ((sent_x, xpeer), (sent_y, ypeer)):
-            flying.append(ship(view(block, h), view(block, h), sem.at[h, n], got_full.at[h, block], "rows", target))
-
-    def climb(h, block, n, upward, downward):
-        for allowed, sems, toward in ((upward, sent_up, PLANE), (downward, sent_down, -PLANE)):
+            flying.append(ship(part, part, sem.at[h, n], got_full.at[h, block], "rows", target))
+
+    def climb(part, got, n, send_up, send_down):
+        zs = visits[n]
+        upward, downward = (zs <= z) & (z < planes - 1), (zs >= z) & (z > 0)
+        for allowed, sem, toward in ((upward, send_up, PLANE), (downward, send_down, -PLANE)):
             @pl.when(allowed)
-            def _(sems=sems, toward=toward):
-                ship(view(block, h), view(block, h), sems.at[h, n], got_full.at[h, block], "rows", me + toward)
-            climbs.append((h, block, n, allowed, sems, toward))
-
-    def await_full(h, block):
-        landed(view(block, h), got_full.at[h, block])
-
-    def absorb(h, *blocks):
-        if h < PARTS - 1:
-            return
-        waiting.extend(blocks)
+            def _(sem=sem, toward=toward):
+                ship(part, part, sem, got, "rows", me + toward)
+            climbs.append((part, got, allowed, sem, toward))
+
+    def settle(h, n, kind, block):
+        key = (n, kind)
+        missing.setdefault(key, PARTS + (1 if n and kind != "q" else 0) * sum(1 for r in TALL if r))
+        missing[key] -= 1
+        if missing[key] == 0:
+            waiting.append(block)
         while len(waiting) >= 2:
             drain(2)
 
@@ -364,40 +372,45 @@
         block = jnp.concatenate([gath[b] for b in taken], axis=0) if n > 1 else gath[taken[0]]
         low[1:2, :] = jnp.minimum(low[1:2, :], column_min(block, points_ref[...]))
 
-    def cross(h, n):
+    def spread_start(h):
+        climb(view(me, h), got_col.at[h, me], 0, sent_up.at[h, 0], sent_down.at[h, 0])
+        pass_on(h, me, 0)
+        settle(h, 0, "q", me)
+
+    def spread_step(h, n):
+        block = visits[n] * PLANE + q
+        landed(view(block, h), got_col.at[h, block])
+        climb(view(block, h), got_col.at[h, block], n, sent_up.at[h, n], sent_down.at[h, n])
+        pass_on(h, block, n)
+        settle(h, n, "q", block)
+
+    def spread_cross(h, n):
         by, bx = visits[n] * PLANE + ypeer % PLANE, visits[n] * PLANE + xpeer % PLANE
-        await_full(h, by)
-        flying.append(ship(
-            view(by, h, upper), view(by, h, upper), sent_dx.at[h, n], got_dx.at[h, by], "rows", xpeer
-        ))
-        await_full(h, bx)
-        flying.append(ship(
-            view(bx, h, lower), view(bx, h, lower), sent_dy.at[h, n], got_dy.at[h, bx], "rows", ypeer
-        ))
-        return by, bx
-
-    def spread_start(h):
-        climb(h, me, 0, z < planes - 1, z > 0)
-        pass_on(h, me, 0)
-        absorb(h, me)
-
-    def spread_step(h, n):
-        zs = visits[n]
-        block = zs * PLANE + q
-        await_full(h, block)
-        climb(h, block, n, (zs < z) & (z < planes - 1), (zs > z) & (z > 0))
-        pass_on(h, block, n)
-        absorb(h, block)
-
-    def spread_cross(h, n):
-        absorb(h, *cross(h, n))
-
-    def spread_rest(h):
-        for zs in visits:
-            bd = zs * PLANE + diag % PLANE
-            landed(view(bd, h, upper), got_dx.at[h, bd])
-            landed(view(bd, h, lower), got_dy.at[h, bd])
-            absorb(h, bd)
+        count, half = flat(h, n), flat(h, n) // 2
+        landed(view(by, h, 0, count), got_full.at[h, by])
+        part = view(by, h, 0, half)
+        flying.append(ship(part, part, sent_dx.at[h, n], got_dx.at[h, by], "rows", xpeer))
+        landed(view(bx, h, 0, count), got_full.at[h, bx])
+        part = view(bx, h, half, half)
+        flying.append(ship(part, part, sent_dy.at[h, n], got_dy.at[h, bx], "rows", ypeer))
+        settle(h, n, "y", by)
+        settle(h, n, "x", bx)
+
+    def spread_diag(h, n):
+        bd, half = visits[n] * PLANE + diag % PLANE, flat(h, n) // 2
+        landed(view(bd, h, 0, half), got_dx.at[h, bd])
+        landed(view(bd, h, half, half), got_dy.at[h, bd])
+        settle(h, n, "d", bd)
+
+    def spread_tall(h, n):
+        for i, (kind, mate) in enumerate((("x", xpeer), ("y", ypeer), ("d", diag))):
+            block = visits[n] * PLANE + mate % PLANE
+            got = got_tall.at[h, block]
+            if n:
+                landed(tall(block, h), got)
+            climb(tall(block, h), got, n, sent_up_tall.at[h, n, i], sent_down_tall.at[h, n, i])
+            if n:
+                settle(h, n, kind, block)
 
     cents_in.wait()
     reduce_cross(0)
@@ -423,21 +436,29 @@
     counts = reduce_own(1)
     renew_own(1, counts)
     spread_start(1)
+    spread_cross(0, 0)
     spread_step(0, 2)
-    spread_cross(0, 0)
     spread_step(1, 1)
+    spread_cross(1, 0)
+    spread_cross(0, 1)
+    spread_diag(1, 0)
+    spread_tall(1, 0)
     spread_step(0, 3)
-    spread_cross(0, 1)
     spread_step(1, 2)
-    spread_cross(1, 0)
     spread_cross(0, 2)
+    spread_tall(1, 1)
+    spread_cross(1, 1)
     spread_step(1, 3)
-    spread_cross(1, 1)
     spread_cross(0, 3)
+    spread_tall(1, 2)
     spread_cross(1, 2)
-    spread_rest(0)
+    for n in range(planes):
+        spread_diag(0, n)
     spread_cross(1, 3)
-    spread_rest(1)
+    spread_diag(1, 1)
+    spread_diag(1, 2)
+    spread_tall(1, 3)
+    spread_diag(1, 3)
     if waiting:
         drain(len(waiting))
 
@@ -445,12 +466,11 @@
     min_copies.append(ship(mine.at[1], theirs.at[1], sent_min.at[1], got_min.at[1], "cent", partner))
     for copy in flying:
         copy.wait_send()
-    for h, block, n, allowed, sems, toward in climbs:
+    for part, got, allowed, sem, toward in climbs:
         @pl.when(allowed)
-        def _(h=h, block=block, n=n, sems=sems, toward=toward):
+        def _(part=part, got=got, sem=sem, toward=toward):
             pltpu.make_async_remote_copy(
-                src_ref=view(block, h), dst_ref=view(block, h), send_sem=sems.at[h, n],
-                recv_sem=got_full.at[h, block], device_id={"rows": me + toward},
+                src_ref=part, dst_ref=part, send_sem=sem, recv_sem=got, device_id={"rows": me + toward}
             ).wait_send()
     for n, copy in enumerate(min_copies):
         copy.wait()
@@ -508,8 +528,9 @@
             pltpu.VMEM((8, count_pts), jnp.float32),
             dma((PARTS, planes, PLANE)), dma((PARTS, planes, PLANE)), dma((PLANE,)), dma((PLANE,)),
             dma((PARTS, hops)), dma((PARTS, hops)), dma((PARTS, hops)), dma((PARTS, hops)),
-            dma((PARTS, planes)), dma((PARTS, planes)), dma((PARTS, planes)), dma((PARTS, planes)),
-            dma((PARTS, rows)),
+            dma((PARTS, planes)), dma((PARTS, planes)), dma((PARTS, rows)),
+            dma((PARTS, planes, 3)), dma((PARTS, planes, 3)), dma((PARTS, rows)),
+            dma((PARTS, planes)), dma((PARTS, planes)), dma((PARTS, rows)),
             dma((PARTS, planes)), dma((PARTS, planes)), dma((PARTS, rows)), dma((PARTS, rows)), dma((1,)),
             dma((2,)), dma((2,)),
         ],

time: 78.8 us -> 79.5 us (level)
  no operation moved by 1% of the time
where the time goes in v4:
time: 79.5 us; the launch traced here: 79.3 us
  Pallas kernels  78.5 us (99%)
  between operations  0.8 us (1%)
    pallas_call x1, Pallas kernels, fused(): pl.pallas_call(functools.partial(lloyd_kernel, rows, cap, share), out_sha...  76.5 us
    pallas_call x1, Pallas kernels, fused(): pl.pallas_call(deliver, out_shape=shapes, in_specs=[vmem, vmem], out_spec...  2.03 us

profile of v4, /device:TPU:0, one launch (start us, length us, event | category | flops | bytes accessed | tf_op | source)
XLA Modules:
  0.0 79.3 jit_solution(13255661224721486478)
XLA Ops:
  0.6 76.5 %shard_map.50 = (f32[2,1024]{1,0:T(2,128)S(1)}, bf16[16,128,1024]{2,1,0:T(8,128)(2,1)S(1)}) custom-call(s32[1,1024]{1,0:T(1,128)} %bitcast.2, bf16[1024,1024]{1,0:T(8,128)(2,1)} %points_hbm.1, bf16[2048,1024]{1,0:T(8,128)(2,1)} %cents_hbm.1), custom_call_target="tpu_custom_call" | custom-call | tf_op jit(solution)/shard_map/pallas_call | solution.py:504
  77.1 2.0 %shard_map.51 = (f32[2,1024]{1,0:T(2,128)}, bf16[16,128,1024]{2,1,0:T(8,128)(2,1)}) custom-call(f32[2,1024]{1,0:T(2,128)S(1)} %get-tuple-element.6.near_ref, bf16[16,128,1024]{2,1,0:T(8,128)(2,1)S(1)} %get-tuple-element.7.gath_ref), custom_call_target="tpu_custom_call" | custom-call | tf_op jit(solution)/shard_map/pallas_call | solution.py:545

commit v5 on v4

--- a/solution.py
+++ b/solution.py
@@ -80,7 +80,7 @@
 LANES = 128
 VMEM_BYTES = 44 * 1024 * 1024
 PARTS = 2
-TALL = (0, 64)
+TALL = (0, 32)
 
 
 def nt_dot(a, b):
@@ -108,7 +108,7 @@
     placing_ref, send, lab_send, arrived, lab_arrived, klab,
     part_send, meta_send, part_got, meta_got, acc, held, mine, theirs, low,
     sent_pts, got_pts, sent_lab, got_lab, sent_part, got_part, sent_meta, got_meta,
-    sent_up, sent_down, got_col, sent_up_tall, sent_down_tall, got_tall, sent_x, sent_y, got_full, sent_dx, sent_dy, got_dx, got_dy, spare_sem, sent_min, got_min,
+    sent_col, got_col, sent_tall, got_tall, sent_x, sent_y, got_full, sent_dx, sent_dy, got_dx, got_dy, spare_sem, sent_min, got_min,
 ):
     count_pts, width = points_ref.shape
     blocksize = cents_ref.shape[0]
@@ -331,7 +331,6 @@
 
     top = z // 2
     visits = [z, z + 1 - 2 * (z % 2), 2 - top, 3 - 3 * top]
-    climbs = []
     waiting = []
     missing = {}
 
@@ -349,14 +348,9 @@
         for sem, target in ((sent_x, xpeer), (sent_y, ypeer)):
             flying.append(ship(part, part, sem.at[h, n], got_full.at[h, block], "rows", target))
 
-    def climb(part, got, n, send_up, send_down):
-        zs = visits[n]
-        upward, downward = (zs <= z) & (z < planes - 1), (zs >= z) & (z > 0)
-        for allowed, sem, toward in ((upward, send_up, PLANE), (downward, send_down, -PLANE)):
-            @pl.when(allowed)
-            def _(sem=sem, toward=toward):
-                ship(part, part, sem, got, "rows", me + toward)
-            climbs.append((part, got, allowed, sem, toward))
+    def climb(part, got, sems):
+        for n in range(1, planes):
+            flying.append(ship(part, part, sems(n), got, "rows", visits[n] * PLANE + q))
 
     def settle(h, n, kind, block):
         key = (n, kind)
@@ -373,14 +367,13 @@
         low[1:2, :] = jnp.minimum(low[1:2, :], column_min(block, points_ref[...]))
 
     def spread_start(h):
-        climb(view(me, h), got_col.at[h, me], 0, sent_up.at[h, 0], sent_down.at[h, 0])
+        climb(view(me, h), got_col.at[h, me], lambda n: sent_col.at[h, n])
         pass_on(h, me, 0)
         settle(h, 0, "q", me)
 
     def spread_step(h, n):
         block = visits[n] * PLANE + q
         landed(view(block, h), got_col.at[h, block])
-        climb(view(block, h), got_col.at[h, block], n, sent_up.at[h, n], sent_down.at[h, n])
         pass_on(h, block, n)
         settle(h, n, "q", block)
 
@@ -408,9 +401,9 @@
             got = got_tall.at[h, block]
             if n:
                 landed(tall(block, h), got)
-            climb(tall(block, h), got, n, sent_up_tall.at[h, n, i], sent_down_tall.at[h, n, i])
-            if n:
                 settle(h, n, kind, block)
+            else:
+                climb(tall(block, h), got, lambda n, i=i: sent_tall.at[h, n, i])
 
     cents_in.wait()
     reduce_cross(0)
@@ -438,24 +431,26 @@
     spread_start(1)
     spread_cross(0, 0)
     spread_step(0, 2)
+    spread_step(0, 3)
     spread_step(1, 1)
     spread_cross(1, 0)
     spread_cross(0, 1)
+    spread_step(1, 2)
     spread_diag(1, 0)
     spread_tall(1, 0)
-    spread_step(0, 3)
-    spread_step(1, 2)
+    spread_step(1, 3)
     spread_cross(0, 2)
+    spread_cross(0, 3)
+    spread_cross(1, 1)
+    spread_diag(0, 0)
+    spread_diag(0, 1)
+    spread_cross(1, 2)
     spread_tall(1, 1)
-    spread_cross(1, 1)
-    spread_step(1, 3)
-    spread_cross(0, 3)
+    spread_diag(0, 2)
+    spread_diag(1, 1)
+    spread_cross(1, 3)
     spread_tall(1, 2)
-    spread_cross(1, 2)
-    for n in range(planes):
-        spread_diag(0, n)
-    spread_cross(1, 3)
-    spread_diag(1, 1)
+    spread_diag(0, 3)
     spread_diag(1, 2)
     spread_tall(1, 3)
     spread_diag(1, 3)
@@ -466,12 +461,6 @@
     min_copies.append(ship(mine.at[1], theirs.at[1], sent_min.at[1], got_min.at[1], "cent", partner))
     for copy in flying:
         copy.wait_send()
-    for part, got, allowed, sem, toward in climbs:
-        @pl.when(allowed)
-        def _(part=part, got=got, sem=sem, toward=toward):
-            pltpu.make_async_remote_copy(
-                src_ref=part, dst_ref=part, send_sem=sem, recv_sem=got, device_id={"rows": me + toward}
-            ).wait_send()
     for n, copy in enumerate(min_copies):
         copy.wait()
         near_ref[n:n + 1, :] = jnp.minimum(mine[n], theirs[n])
@@ -528,8 +517,7 @@
             pltpu.VMEM((8, count_pts), jnp.float32),
             dma((PARTS, planes, PLANE)), dma((PARTS, planes, PLANE)), dma((PLANE,)), dma((PLANE,)),
             dma((PARTS, hops)), dma((PARTS, hops)), dma((PARTS, hops)), dma((PARTS, hops)),
-            dma((PARTS, planes)), dma((PARTS, planes)), dma((PARTS, rows)),
-            dma((PARTS, planes, 3)), dma((PARTS, planes, 3)), dma((PARTS, rows)),
+            dma((PARTS, planes)), dma((PARTS, rows)), dma((PARTS, planes, 3)), dma((PARTS, rows)),
             dma((PARTS, planes)), dma((PARTS, planes)), dma((PARTS, rows)),
             dma((PARTS, planes)), dma((PARTS, planes)), dma((PARTS, rows)), dma((PARTS, rows)), dma((1,)),
             dma((2,)), dma((2,)),

time: 79.5 us -> 79.4 us (level)
  no operation moved by 1% of the time
where the time goes in v5:
time: 79.4 us; the launch traced here: 79.2 us
  Pallas kernels  78.4 us (99%)
  between operations  0.8 us (1%)
    pallas_call x1, Pallas kernels, fused(): pl.pallas_call(functools.partial(lloyd_kernel, rows, cap, share), out_sha...  76.4 us
    pallas_call x1, Pallas kernels, fused(): pl.pallas_call(deliver, out_shape=shapes, in_specs=[vmem, vmem], out_spec...  2.03 us

profile of v5, /device:TPU:0, one launch (start us, length us, event | category | flops | bytes accessed | tf_op | source)
XLA Modules:
  0.0 79.2 jit_solution(4911725309927918821)
XLA Ops:
  0.6 76.4 %shard_map.50 = (f32[2,1024]{1,0:T(2,128)S(1)}, bf16[16,128,1024]{2,1,0:T(8,128)(2,1)S(1)}) custom-call(s32[1,1024]{1,0:T(1,128)} %bitcast.2, bf16[1024,1024]{1,0:T(8,128)(2,1)} %points_hbm.1, bf16[2048,1024]{1,0:T(8,128)(2,1)} %cents_hbm.1), custom_call_target="tpu_custom_call" | custom-call | tf_op jit(solution)/shard_map/pallas_call | solution.py:493
  77.0 2.0 %shard_map.51 = (f32[2,1024]{1,0:T(2,128)}, bf16[16,128,1024]{2,1,0:T(8,128)(2,1)}) custom-call(f32[2,1024]{1,0:T(2,128)S(1)} %get-tuple-element.6.near_ref, bf16[16,128,1024]{2,1,0:T(8,128)(2,1)S(1)} %get-tuple-element.7.gath_ref), custom_call_target="tpu_custom_call" | custom-call | tf_op jit(solution)/shard_map/pallas_call | solution.py:533

commit v6 on v2

--- a/solution.py
+++ b/solution.py
@@ -80,6 +80,7 @@
 LANES = 128
 VMEM_BYTES = 44 * 1024 * 1024
 PARTS = 2
+TALL = (0, 0)
 
 
 def nt_dot(a, b):
@@ -105,9 +106,9 @@
     rows, cap, share, assign_hbm, points_hbm, cents_hbm, near_ref, gath,
     assign_ref, points_ref, cents_ref, load_sem,
     placing_ref, send, lab_send, arrived, lab_arrived, klab,
-    part_send, meta_send, part_got, meta_got, acc, mine, theirs, low,
-    sent_pts, got_pts, sent_lab, got_lab, sent_part, got_part, sent_meta, got_meta,
-    sent_up, sent_down, sent_x, sent_y, got_full, sent_dx, sent_dy, got_dx, got_dy, spare_sem, sent_min, got_min,
+    part_send, meta_send, part_got, meta_got, part_in, meta_in, held, tally, mine, theirs, low,
+    sent_pts, got_pts, sent_lab, got_lab, sent_part, got_part, sent_meta, got_in,
+    sent_gath, sent_col, sent_tall, got_col, got_tall, got_side, got_diag, spare_sem, sent_min, got_min,
 ):
     count_pts, width = points_ref.shape
     blocksize = cents_ref.shape[0]
@@ -152,8 +153,10 @@
         pieces.append(jnp.sum(part * before, axis=0, keepdims=True))
         carry = carry + jnp.sum(part, axis=1, keepdims=True)
     ranking = jnp.concatenate(pieces, axis=1)
-    plane_to = jnp.floor(owner * (1.0 / PLANE))
-    slot = jnp.where(inside, (owner - plane_to * PLANE) * chunk + plane_to * cap + ranking, -1.0)
+    side_to = jnp.floor(owner * (1.0 / (2 * PLANE)))
+    pair_to = jnp.floor(owner * 0.5)
+    column_to, lane_to = pair_to - side_to * PLANE, side_to * 2.0 + owner - pair_to * 2.0
+    slot = jnp.where(inside, column_to * chunk + lane_to * cap + ranking, -1.0)
     labels8 = jnp.broadcast_to(offset1, (8, count_pts)).astype(jnp.bfloat16)
 
     def ship(src, dst, ss, rs, axis, target):
@@ -168,9 +171,17 @@
             src_ref=ref, dst_ref=ref, send_sem=spare_sem.at[0], recv_sem=sem, device_id={"rows": xpeer}
         ).wait_recv()
 
-    flying = []
+    def sent_all(ref, sem):
+        pltpu.make_async_remote_copy(
+            src_ref=ref, dst_ref=ref, send_sem=sem, recv_sem=spare_sem.at[0], device_id={"rows": xpeer}
+        ).wait_send()
+
     reach = (3, 1, 2)
-    span = (2, 3, 1)
+    side = z // 2
+    inner = (z > 0) & (z < planes - 1)
+    outer = jnp.logical_not(inner)
+    beside, across = flip(z, 1) * PLANE + q, (planes - 1 - z) * PLANE + q
+    order = (2 - 2 * side, 3 - 2 * side, 2 * side, 2 * side + 1)
 
     def place(k):
         i = flip(q, k)
@@ -198,27 +209,28 @@
                 arrived[h, t, pl.ds(pl.multiple_of(q * cap, cap), cap), :] = rows_out[t * cap:(t + 1) * cap]
 
     def dispatch(h, j, k):
-        t = flip(z, (span + (0,))[j])
+        t = order[j]
         spot = pl.ds(pl.multiple_of(q * cap, cap), cap)
-        flying.append(ship(
+        ship(
             send.at[h, k, pl.ds(pl.multiple_of(t * cap, cap), cap)], arrived.at[h, t, spot],
-            sent_pts.at[h, j, k], got_pts.at[h, t, q], "rows", z * PLANE + flip(q, k),
-        ))
-
+            sent_pts.at[0], got_pts.at[h, t], "rows", z * PLANE + flip(q, k),
+        )
+
+    place(reach[0])
     points_in.wait()
     cents_in = pltpu.make_async_copy(cents_hbm, cents_ref, load_sem.at[1])
     cents_in.start()
     for k in reach:
-        place(k)
+        if k != reach[0]:
+            place(k)
         fill(0, k)
         if k == reach[0]:
             pl.semaphore_wait(barrier, 7)
-        flying.append(ship(
-            lab_send.at[k], lab_arrived.at[q], sent_lab.at[k], got_lab.at[q], "rows", z * PLANE + flip(q, k)
-        ))
-        for j in range(planes // 2):
-            dispatch(0, j, k)
-    for j in range(planes // 2, planes):
+        ship(
+            lab_send.at[k], lab_arrived.at[q], sent_lab.at[0], got_lab.at[0], "rows", z * PLANE + flip(q, k)
+        )
+        dispatch(0, 0, k)
+    for j in range(1, planes):
         for k in reach:
             dispatch(0, j, k)
     for h in range(1, PARTS):
@@ -246,8 +258,7 @@
         ones = jnp.ones((8, width), jnp.bfloat16)
         return (nt_dot(ones, high) + nt_dot(ones, rest))[0:1, :]
 
-    for k in reach:
-        landed(lab_arrived.at[flip(q, k)], got_lab.at[flip(q, k)])
+    landed(lab_arrived.at[0:PLANE - 1], got_lab.at[0])
     lane = lax.broadcasted_iota(jnp.int32, (8, LANES), 1)
     for t in range(planes):
         for p in range(PLANE // 2):
@@ -270,17 +281,13 @@
         return jnp.sum(jnp.where(eye, row, 0.0), axis=1, keepdims=True)
 
     def gather_in(h, t):
-        for k in reach:
-            source = flip(q, k)
-            landed(arrived.at[h, t, pl.ds(pl.multiple_of(source * cap, cap), cap)], got_pts.at[h, t, source])
+        landed(arrived.at[h, t, 0:(PLANE - 1) * cap], got_pts.at[h, t])
         chosen = jnp.where(rowid1 == klab[t][0:1, :], 1.0, 0.0)
         counts = jnp.sum(chosen, axis=1, keepdims=True)
         total = jnp.dot(chosen.astype(jnp.bfloat16), arrived[h, t], preferred_element_type=jnp.float32)
         return total, counts
 
-    def reduce_out(h, j):
-        t = flip(z, span[j])
-        total, counts = gather_in(h, t)
+    def send_part(h, j, total, counts, part_to, meta_to, got, target):
         peak = jnp.maximum(jnp.max(jnp.abs(total), axis=1, keepdims=True), 1e-30)
         grow = jnp.exp2(14.0 - jnp.floor(jnp.log2(peak)))
         grow = jnp.where(peak * grow >= 32767.0, grow * 0.5, grow)
@@ -288,144 +295,229 @@
         part_send[h, j] = scaled.astype(jnp.int32).astype(jnp.int16)
         first_row = lax.broadcasted_iota(jnp.int32, (8, LANES), 0) == 0
         meta_send[h, j] = jnp.where(first_row, to_row(1.0 / grow), to_row(counts))
-        target = t * PLANE + q
-        flying.append(ship(
-            meta_send.at[h, j], meta_got.at[h, z], sent_meta.at[h, j], got_meta.at[h, z], "rows", target
-        ))
-        flying.append(ship(
-            part_send.at[h, j], part_got.at[h, z], sent_part.at[h, j], got_part.at[h, z], "rows", target
-        ))
-
-    def reduce_own(h):
-        total, counts = gather_in(h, z)
-        own_rows = cents_ref[pl.ds(pl.multiple_of(me * share, share), share), h * wide:(h + 1) * wide]
-        acc[h] = total + own_rows.astype(jnp.float32)
-        return counts
-
-    def renew_own(h, counts):
-        for bits in (1, 2, 3):
-            t = flip(z, bits)
-            landed(meta_got.at[h, t], got_meta.at[h, t])
-            landed(part_got.at[h, t], got_part.at[h, t])
-            meta = meta_got[h, t]
-            counts = counts + to_column(meta[1:2, :])
-            acc[h] += part_got[h, t].astype(jnp.int32).astype(jnp.float32) * to_column(meta[0:1, :])
-        gath[me, :, h * wide:(h + 1) * wide] = (acc[h] / (counts + 1.0)).astype(jnp.bfloat16)
-
-    half = share // 2
-    upper, lower = pl.ds(0, half), pl.ds(half, half)
-    top = z // 2
-    visits = [z, z + 1 - 2 * (z % 2), 2 - top, 3 - 3 * top]
-    climbs = []
-    waiting = []
-
-    def view(block, h, part=slice(None)):
-        return gath.at[block, part, h * wide:(h + 1) * wide]
-
-    def pass_on(h, block, n):
-        for sem, target in ((sent_x, xpeer), (sent_y, ypeer)):
-            flying.append(ship(view(block, h), view(block, h), sem.at[h, n], got_full.at[h, block], "rows", target))
-
-    def climb(h, block, n, upward, downward):
-        for allowed, sems, toward in ((upward, sent_up, PLANE), (downward, sent_down, -PLANE)):
-            @pl.when(allowed)
-            def _(sems=sems, toward=toward):
-                ship(view(block, h), view(block, h), sems.at[h, n], got_full.at[h, block], "rows", me + toward)
-            climbs.append((h, block, n, allowed, sems, toward))
-
-    def await_full(h, block):
-        landed(view(block, h), got_full.at[h, block])
-
-    def absorb(h, *blocks):
-        if h < PARTS - 1:
-            return
-        waiting.extend(blocks)
-        while len(waiting) >= 2:
-            drain(2)
-
-    def drain(n):
-        taken, waiting[:] = waiting[:n], waiting[n:]
-        block = jnp.concatenate([gath[b] for b in taken], axis=0) if n > 1 else gath[taken[0]]
-        low[1:2, :] = jnp.minimum(low[1:2, :], column_min(block, points_ref[...]))
-
-    def cross(h, n):
-        by, bx = visits[n] * PLANE + ypeer % PLANE, visits[n] * PLANE + xpeer % PLANE
-        await_full(h, by)
-        flying.append(ship(
-            view(by, h, upper), view(by, h, upper), sent_dx.at[h, n], got_dx.at[h, by], "rows", xpeer
-        ))
-        await_full(h, bx)
-        flying.append(ship(
-            view(bx, h, lower), view(bx, h, lower), sent_dy.at[h, n], got_dy.at[h, bx], "rows", ypeer
-        ))
-        return by, bx
-
-    def spread_start(h):
-        climb(h, me, 0, z < planes - 1, z > 0)
-        pass_on(h, me, 0)
-        absorb(h, me)
-
-    def spread_step(h, n):
-        zs = visits[n]
-        block = zs * PLANE + q
-        await_full(h, block)
-        climb(h, block, n, (zs < z) & (z < planes - 1), (zs > z) & (z > 0))
-        pass_on(h, block, n)
-        ready = cross(h, n - 1)
-        absorb(h, block, *ready)
-
-    def spread_end(h):
-        absorb(h, *cross(h, planes - 1))
-
-    def spread_rest(h):
-        for zs in visits:
-            bd = zs * PLANE + diag % PLANE
-            landed(view(bd, h, upper), got_dx.at[h, bd])
-            landed(view(bd, h, lower), got_dy.at[h, bd])
-            absorb(h, bd)
+        ship(meta_send.at[h, j], meta_to, sent_meta.at[0], got.at[1], "rows", target)
+        ship(part_send.at[h, j], part_to, sent_part.at[0], got.at[0], "rows", target)
+
+    def take_part(part_from, meta_from, got):
+        landed(meta_from, got.at[1])
+        landed(part_from, got.at[0])
+        meta = meta_from[...]
+        return part_from[...].astype(jnp.int32).astype(jnp.float32) * to_column(meta[0:1, :]), to_column(meta[1:2, :])
+
+    def reduce_in(h, j):
+        t = order[j]
+        total, counts = gather_in(h, t)
+
+        @pl.when(outer)
+        def _():
+            send_part(h, j, total, counts, part_got.at[h, t], meta_got.at[h, t], got_part.at[h, t], beside)
+
+        @pl.when(inner)
+        def _():
+            held[h, j] = total
+            tally[h, j] = counts
+
+    def reduce_far(h, j):
+        @pl.when(inner)
+        def _():
+            t = order[j]
+            more, extra = take_part(part_got.at[h, t], meta_got.at[h, t], got_part.at[h, t])
+            send_part(
+                h, j, held[h, j] + more, tally[h, j] + extra, part_in.at[h, j], meta_in.at[h, j], got_in.at[h, j], across
+            )
+
+    def renew(h):
+        @pl.when(inner)
+        def _():
+            for p in range(2):
+                block, t = side * 2 * PLANE + 2 * q + p, order[2 + p]
+                rows_own = cents_ref[pl.ds(pl.multiple_of(block * share, share), share), h * wide:(h + 1) * wide]
+                total, counts = held[h, 2 + p] + rows_own.astype(jnp.float32), tally[h, 2 + p]
+                more, extra = take_part(part_got.at[h, t], meta_got.at[h, t], got_part.at[h, t])
+                total, counts = total + more, counts + extra
+                more, extra = take_part(part_in.at[h, p], meta_in.at[h, p], got_in.at[h, p])
+                total, counts = total + more, counts + extra
+                gath[block, :, h * wide:(h + 1) * wide] = (total / (counts + 1.0)).astype(jnp.bfloat16)
+
+    waiting = {}
+
+    def sides(n):
+        return (side, 1 - side)[n]
+
+    def cols(h):
+        return slice(h * wide, (h + 1) * wide)
+
+    def pair(h, n, mate, first=0, count=share):
+        return gath.at[pl.ds(sides(n) * 2 * PLANE + 2 * (mate % PLANE), 2), pl.ds(first, count), cols(h)]
+
+    def one(h, n, p):
+        return gath.at[sides(n) * 2 * PLANE + 2 * q + p, :, cols(h)]
+
+    def pile(h, blocks, count):
+        return gath.at[0:blocks, pl.ds(0, count), cols(h)]
+
+    def flat(h, n, within):
+        return share if within and n == 0 else share - TALL[h]
+
+    def by_role(body):
+        @pl.when(inner)
+        def _():
+            body(True)
+
+        @pl.when(outer)
+        def _():
+            body(False)
+
+    def settle(h, n, kind, mate):
+        key = (n, kind)
+        waiting.setdefault(key, PARTS + (0 if kind == "q" else sum(1 for r in TALL if r)))
+        waiting[key] -= 1
+        if waiting[key] == 0:
+            first = sides(n) * 2 * PLANE + 2 * (mate % PLANE)
+            block = jnp.concatenate([gath[first], gath[first + 1]], axis=0)
+            low[1:2, :] = jnp.minimum(low[1:2, :], column_min(block, points_ref[...]))
+
+    def pass_on(h, n, count):
+        part = pair(h, n, me, 0, count)
+        for target in (xpeer, ypeer):
+            ship(part, part, sent_gath.at[h], got_side.at[h, n], "rows", target)
+
+    def start_inner(h):
+        @pl.when(inner)
+        def _():
+            for p in range(2):
+                ship(one(h, 0, p), one(h, 0, p), sent_col.at[h], got_col.at[h, 1, p], "rows", across)
+                ship(one(h, 0, p), one(h, 0, p), sent_col.at[h], got_col.at[h, 0, p], "rows", beside)
+            pass_on(h, 0, share)
+
+    def start_outer(h):
+        @pl.when(outer)
+        def _():
+            for p in range(2):
+                landed(one(h, 0, p), got_col.at[h, 0, p])
+            pass_on(h, 0, flat(h, 0, False))
+        settle(h, 0, "q", me)
+
+    def next_inner(h):
+        @pl.when(inner)
+        def _():
+            for p in range(2):
+                landed(one(h, 1, p), got_col.at[h, 1, p])
+                ship(one(h, 1, p), one(h, 1, p), sent_col.at[h], got_col.at[h, 1, p], "rows", beside)
+            pass_on(h, 1, flat(h, 1, True))
+
+    def next_outer(h):
+        @pl.when(outer)
+        def _():
+            for p in range(2):
+                landed(one(h, 1, p), got_col.at[h, 1, p])
+            pass_on(h, 1, flat(h, 1, False))
+        settle(h, 1, "q", me)
+
+    def spread_cross(h, n):
+        def body(within):
+            count = flat(h, n, within)
+            landed(pile(h, 4, count), got_side.at[h, n])
+            for mate, first, target in ((ypeer, 0, xpeer), (xpeer, count // 2, ypeer)):
+                part = pair(h, n, mate, first, count // 2)
+                ship(part, part, sent_gath.at[h], got_diag.at[h, n], "rows", target)
+        if n == 0 and TALL[h]:
+            by_role(body)
+        else:
+            body(False)
+        settle(h, n, "y", ypeer)
+        settle(h, n, "x", xpeer)
+
+    def spread_diag(h, n):
+        def body(within):
+            landed(pile(h, 2, flat(h, n, within)), got_diag.at[h, n])
+        if n == 0 and TALL[h]:
+            by_role(body)
+        else:
+            body(False)
+        settle(h, n, "d", diag)
+
+    def spread_tall(h, n):
+        count = TALL[h]
+        if n == 0:
+            @pl.when(outer)
+            def _():
+                landed(pile(h, 6, count), got_tall.at[h, 0])
+        else:
+            landed(pile(h, 6, count), got_tall.at[h, 1])
+
+        @pl.when(inner)
+        def _():
+            for mate in (xpeer, ypeer, diag):
+                part = pair(h, n, mate, share - count, count)
+                if n == 0:
+                    ship(part, part, sent_tall.at[h], got_tall.at[h, 1], "rows", across)
+                ship(part, part, sent_tall.at[h], got_tall.at[h, n], "rows", beside)
+        for kind, mate in (("x", xpeer), ("y", ypeer), ("d", diag)):
+            settle(h, n, kind, mate)
 
     cents_in.wait()
-    for j in range(planes - 1):
-        reduce_out(0, j)
-        first_piece(j)
-    counts = reduce_own(0)
+    reduce_in(0, 0)
+    first_piece(0)
+    reduce_in(0, 1)
+    first_piece(1)
+    reduce_far(0, 0)
+    reduce_in(0, 2)
+    first_piece(2)
+    reduce_far(0, 1)
+    reduce_in(0, 3)
     for i in range(planes - 1, pieces_first):
         first_piece(i)
-    reduce_out(1, 0)
-    renew_own(0, counts)
-    spread_start(0)
-    reduce_out(1, 1)
+    renew(0)
+    start_inner(0)
+    reduce_in(1, 0)
     pnorm = point_norms()
     mine[0] = (pnorm + low[0:1, :]) / width
     min_copies.append(ship(mine.at[0], theirs.at[0], sent_min.at[0], got_min.at[0], "cent", partner))
-    reduce_out(1, 2)
-    spread_step(0, 1)
-    counts = reduce_own(1)
-    renew_own(1, counts)
-    spread_start(1)
-    spread_step(0, 2)
-    spread_step(1, 1)
-    spread_step(0, 3)
-    spread_step(1, 2)
-    spread_end(0)
-    spread_step(1, 3)
-    spread_rest(0)
-    spread_end(1)
-    spread_rest(1)
-    if waiting:
-        drain(len(waiting))
+    reduce_in(1, 1)
+    reduce_far(1, 0)
+    reduce_in(1, 2)
+    reduce_far(1, 1)
+    next_inner(0)
+    start_outer(0)
+    reduce_in(1, 3)
+    renew(1)
+    start_inner(1)
+    next_outer(0)
+    spread_cross(0, 0)
+    spread_cross(0, 1)
+    next_inner(1)
+    start_outer(1)
+    next_outer(1)
+    spread_cross(1, 0)
+    spread_cross(1, 1)
+    spread_diag(0, 0)
+    spread_diag(0, 1)
+    spread_diag(1, 0)
+    spread_diag(1, 1)
 
     mine[1] = (pnorm + low[1:2, :]) / width
     min_copies.append(ship(mine.at[1], theirs.at[1], sent_min.at[1], got_min.at[1], "cent", partner))
-    for copy in flying:
-        copy.wait_send()
-    for h, block, n, allowed, sems, toward in climbs:
-        @pl.when(allowed)
-        def _(h=h, block=block, n=n, sems=sems, toward=toward):
-            pltpu.make_async_remote_copy(
-                src_ref=view(block, h), dst_ref=view(block, h), send_sem=sems.at[h, n],
-                recv_sem=got_full.at[h, block], device_id={"rows": me + toward},
-            ).wait_send()
+    sent_all(send.at[:, 1:], sent_pts.at[0])
+    sent_all(lab_send.at[1:], sent_lab.at[0])
+
+    @pl.when(outer)
+    def _():
+        sent_all(part_send, sent_part.at[0])
+        sent_all(meta_send, sent_meta.at[0])
+        for h in range(PARTS):
+            sent_all(pile(h, 3 * PLANE, flat(h, 0, False)), sent_gath.at[h])
+
+    @pl.when(inner)
+    def _():
+        sent_all(part_send.at[:, 0:2], sent_part.at[0])
+        sent_all(meta_send.at[:, 0:2], sent_meta.at[0])
+        for h in range(PARTS):
+            sent_all(pile(h, 3 * PLANE, (share + flat(h, 1, True)) // 2), sent_gath.at[h])
+            sent_all(pile(h, 6, share), sent_col.at[h])
+            if TALL[h]:
+                sent_all(pile(h, 9, 2 * TALL[h]), sent_tall.at[h])
+
     for n, copy in enumerate(min_copies):
         copy.wait()
         near_ref[n:n + 1, :] = jnp.minimum(mine[n], theirs[n])
@@ -454,7 +546,6 @@
         jax.ShapeDtypeStruct((2, count_pts), jnp.float32),
         jax.ShapeDtypeStruct((rows, share, width), jnp.bfloat16),
     )
-    hops = planes - 1
     near, upd = pl.pallas_call(
         functools.partial(lloyd_kernel, rows, cap, share),
         out_shape=shapes,
@@ -471,20 +562,22 @@
             pltpu.VMEM((PARTS, planes, PLANE * cap, wide), jnp.bfloat16),
             pltpu.VMEM((PLANE, chunk // LANES, 8, LANES), jnp.float32),
             pltpu.VMEM((planes, 8, PLANE * cap), jnp.float32),
-            pltpu.VMEM((PARTS, hops, share, wide), jnp.int16),
-            pltpu.VMEM((PARTS, hops, 8, LANES), jnp.float32),
             pltpu.VMEM((PARTS, planes, share, wide), jnp.int16),
             pltpu.VMEM((PARTS, planes, 8, LANES), jnp.float32),
-            pltpu.VMEM((PARTS, share, wide), jnp.float32),
+            pltpu.VMEM((PARTS, planes, share, wide), jnp.int16),
+            pltpu.VMEM((PARTS, planes, 8, LANES), jnp.float32),
+            pltpu.VMEM((PARTS, 2, share, wide), jnp.int16),
+            pltpu.VMEM((PARTS, 2, 8, LANES), jnp.float32),
+            pltpu.VMEM((PARTS, planes, share, wide), jnp.float32),
+            pltpu.VMEM((PARTS, planes, share, 1), jnp.float32),
             pltpu.VMEM((2, 1, count_pts), jnp.float32),
             pltpu.VMEM((2, 1, count_pts), jnp.float32),
             pltpu.VMEM((8, count_pts), jnp.float32),
-            dma((PARTS, planes, PLANE)), dma((PARTS, planes, PLANE)), dma((PLANE,)), dma((PLANE,)),
-            dma((PARTS, hops)), dma((PARTS, planes)), dma((PARTS, hops)), dma((PARTS, planes)),
-            dma((PARTS, planes)), dma((PARTS, planes)), dma((PARTS, planes)), dma((PARTS, planes)),
-            dma((PARTS, rows)),
-            dma((PARTS, planes)), dma((PARTS, planes)), dma((PARTS, rows)), dma((PARTS, rows)), dma((1,)),
-            dma((2,)), dma((2,)),
+            dma((1,)), dma((PARTS, planes)), dma((1,)), dma((1,)),
+            dma((1,)), dma((PARTS, planes, 2)), dma((1,)), dma((PARTS, 2, 2)),
+            dma((PARTS,)), dma((PARTS,)), dma((PARTS,)),
+            dma((PARTS, 2, 2)), dma((PARTS, 2)), dma((PARTS, 2)), dma((PARTS, 2)),
+            dma((1,)), dma((2,)), dma((2,)),
         ],
         compiler_params=pltpu.CompilerParams(
             collective_id=0, has_side_effects=True, vmem_limit_bytes=VMEM_BYTES

time: 80.5 us -> 73.8 us (0.917)
  Pallas kernels: 79.5 us -> 72.9 us
    pallas_call x1, Pallas kernels: 77.5 us -> 70.8 us  [fused(): pl.pallas_call(functools.partial(lloyd_kernel, rows, cap, share), out_sha...]
where the time goes in v6:
time: 73.8 us; the launch traced here: 73.6 us
  Pallas kernels  72.9 us (99%)
  between operations  0.8 us (1%)
    pallas_call x1, Pallas kernels, fused(): pl.pallas_call(functools.partial(lloyd_kernel, rows, cap, share), out_sha...  70.8 us
    pallas_call x1, Pallas kernels, fused(): pl.pallas_call(deliver, out_shape=shapes, in_specs=[vmem, vmem], out_spec...  2.03 us

profile of v6, /device:TPU:0, one launch (start us, length us, event | category | flops | bytes accessed | tf_op | source)
XLA Modules:
  0.0 73.6 jit_solution(3669406253830504611)
XLA Ops:
  0.6 70.8 %shard_map.50 = (f32[2,1024]{1,0:T(2,128)S(1)}, bf16[16,128,1024]{2,1,0:T(8,128)(2,1)S(1)}) custom-call(s32[1,1024]{1,0:T(1,128)} %bitcast.2, bf16[1024,1024]{1,0:T(8,128)(2,1)} %points_hbm.1, bf16[2048,1024]{1,0:T(8,128)(2,1)} %cents_hbm.1), custom_call_target="tpu_custom_call" | custom-call | tf_op jit(solution)/shard_map/pallas_call | solution.py:549
  71.5 2.0 %shard_map.51 = (f32[2,1024]{1,0:T(2,128)}, bf16[16,128,1024]{2,1,0:T(8,128)(2,1)}) custom-call(f32[2,1024]{1,0:T(2,128)S(1)} %get-tuple-element.6.near_ref, bf16[16,128,1024]{2,1,0:T(8,128)(2,1)S(1)} %get-tuple-element.7.gath_ref), custom_call_target="tpu_custom_call" | custom-call | tf_op jit(solution)/shard_map/pallas_call | solution.py:590

commit v7 on v6

--- a/solution.py
+++ b/solution.py
@@ -80,7 +80,7 @@
 LANES = 128
 VMEM_BYTES = 44 * 1024 * 1024
 PARTS = 2
-TALL = (0, 0)
+TALL = ((64, 32), (0, 0))
 
 
 def nt_dot(a, b):
@@ -339,8 +339,6 @@
                 total, counts = total + more, counts + extra
                 gath[block, :, h * wide:(h + 1) * wide] = (total / (counts + 1.0)).astype(jnp.bfloat16)
 
-    waiting = {}
-
     def sides(n):
         return (side, 1 - side)[n]
 
@@ -350,111 +348,99 @@
     def pair(h, n, mate, first=0, count=share):
         return gath.at[pl.ds(sides(n) * 2 * PLANE + 2 * (mate % PLANE), 2), pl.ds(first, count), cols(h)]
 
-    def one(h, n, p):
-        return gath.at[sides(n) * 2 * PLANE + 2 * q + p, :, cols(h)]
+    def one(h, n, mate, p, first=0, count=share):
+        return gath.at[sides(n) * 2 * PLANE + 2 * (mate % PLANE) + p, pl.ds(first, count), cols(h)]
 
     def pile(h, blocks, count):
         return gath.at[0:blocks, pl.ds(0, count), cols(h)]
 
     def flat(h, n, within):
-        return share if within and n == 0 else share - TALL[h]
-
-    def by_role(body):
-        @pl.when(inner)
-        def _():
-            body(True)
-
-        @pl.when(outer)
-        def _():
-            body(False)
-
-    def settle(h, n, kind, mate):
-        key = (n, kind)
-        waiting.setdefault(key, PARTS + (0 if kind == "q" else sum(1 for r in TALL if r)))
-        waiting[key] -= 1
-        if waiting[key] == 0:
-            first = sides(n) * 2 * PLANE + 2 * (mate % PLANE)
-            block = jnp.concatenate([gath[first], gath[first + 1]], axis=0)
-            low[1:2, :] = jnp.minimum(low[1:2, :], column_min(block, points_ref[...]))
-
-    def pass_on(h, n, count):
-        part = pair(h, n, me, 0, count)
-        for target in (xpeer, ypeer):
-            ship(part, part, sent_gath.at[h], got_side.at[h, n], "rows", target)
-
-    def start_inner(h):
-        @pl.when(inner)
-        def _():
-            for p in range(2):
-                ship(one(h, 0, p), one(h, 0, p), sent_col.at[h], got_col.at[h, 1, p], "rows", across)
-                ship(one(h, 0, p), one(h, 0, p), sent_col.at[h], got_col.at[h, 0, p], "rows", beside)
-            pass_on(h, 0, share)
-
-    def start_outer(h):
-        @pl.when(outer)
-        def _():
-            for p in range(2):
-                landed(one(h, 0, p), got_col.at[h, 0, p])
-            pass_on(h, 0, flat(h, 0, False))
-        settle(h, 0, "q", me)
-
-    def next_inner(h):
-        @pl.when(inner)
-        def _():
-            for p in range(2):
-                landed(one(h, 1, p), got_col.at[h, 1, p])
-                ship(one(h, 1, p), one(h, 1, p), sent_col.at[h], got_col.at[h, 1, p], "rows", beside)
-            pass_on(h, 1, flat(h, 1, True))
-
-    def next_outer(h):
-        @pl.when(outer)
-        def _():
-            for p in range(2):
-                landed(one(h, 1, p), got_col.at[h, 1, p])
-            pass_on(h, 1, flat(h, 1, False))
-        settle(h, 1, "q", me)
-
-    def spread_cross(h, n):
-        def body(within):
-            count = flat(h, n, within)
-            landed(pile(h, 4, count), got_side.at[h, n])
+        if within:
+            return share - TALL[h][0] * n
+        return share - TALL[h][1]
+
+    def pass_on(h, n, within):
+        for p in range(2):
+            part = one(h, n, me, p, 0, flat(h, n, within))
+            for target in (xpeer, ypeer):
+                ship(part, part, sent_gath.at[h], got_side.at[h, n, p], "rows", target)
+
+    def own_start(h):
+        for p in range(2):
+            part = one(h, 0, me, p)
+            ship(part, part, sent_col.at[h], got_col.at[h, 1, p], "rows", across)
+            ship(part, part, sent_col.at[h], got_col.at[h, 0, p], "rows", beside)
+
+    def column_in(h, n, within):
+        for p in range(2):
+            part = one(h, n, me, p)
+            landed(part, got_col.at[h, n, p])
+            if within:
+                ship(part, part, sent_col.at[h], got_col.at[h, n, p], "rows", beside)
+
+    def cross(h, n, within):
+        count = flat(h, n, within)
+        for p in range(2):
+            landed(pile(h, 2, count), got_side.at[h, n, p])
             for mate, first, target in ((ypeer, 0, xpeer), (xpeer, count // 2, ypeer)):
-                part = pair(h, n, mate, first, count // 2)
+                part = one(h, n, mate, p, first, count // 2)
                 ship(part, part, sent_gath.at[h], got_diag.at[h, n], "rows", target)
-        if n == 0 and TALL[h]:
-            by_role(body)
-        else:
-            body(False)
-        settle(h, n, "y", ypeer)
-        settle(h, n, "x", xpeer)
-
-    def spread_diag(h, n):
-        def body(within):
-            landed(pile(h, 2, flat(h, n, within)), got_diag.at[h, n])
-        if n == 0 and TALL[h]:
-            by_role(body)
-        else:
-            body(False)
-        settle(h, n, "d", diag)
-
-    def spread_tall(h, n):
-        count = TALL[h]
-        if n == 0:
-            @pl.when(outer)
-            def _():
-                landed(pile(h, 6, count), got_tall.at[h, 0])
-        else:
-            landed(pile(h, 6, count), got_tall.at[h, 1])
-
-        @pl.when(inner)
-        def _():
+
+    def spread_tall(h, n, within):
+        near, far = TALL[h][1], TALL[h][0]
+        if not within or n:
+            landed(pile(h, 6, far if within else near), got_tall.at[h, n])
+        if within:
             for mate in (xpeer, ypeer, diag):
-                part = pair(h, n, mate, share - count, count)
                 if n == 0:
+                    part = pair(h, n, mate, share - far, far)
                     ship(part, part, sent_tall.at[h], got_tall.at[h, 1], "rows", across)
-                ship(part, part, sent_tall.at[h], got_tall.at[h, n], "rows", beside)
-        for kind, mate in (("x", xpeer), ("y", ypeer), ("d", diag)):
-            settle(h, n, kind, mate)
+            if n:
+                tall_out(h, n)
+
+    def tall_out(h, n):
+        near = TALL[h][1]
+        for mate in (xpeer, ypeer, diag):
+            part = pair(h, n, mate, share - near, near)
+            ship(part, part, sent_tall.at[h], got_tall.at[h, n], "rows", beside)
+
+    def run(within, steps):
+        missing = {}
+        for n in range(2):
+            missing[n, "q"] = 1 + (n and not within)
+            for kind in "xyd":
+                missing[n, kind] = PARTS + (0 if within and n == 0 else sum(1 for r in TALL if r[0]))
+
+        def settle(n, kinds):
+            for kind in kinds:
+                missing[n, kind] -= 1
+                if missing[n, kind] == 0:
+                    mate = {"q": me, "x": xpeer, "y": ypeer, "d": diag}[kind]
+                    first = sides(n) * 2 * PLANE + 2 * (mate % PLANE)
+                    block = jnp.concatenate([gath[first], gath[first + 1]], axis=0)
+                    low[1:2, :] = jnp.minimum(low[1:2, :], column_min(block, points_ref[...]))
+
+        for what, h, n in steps:
+            if what == "S":
+                own_start(h)
+                settle(n, "q")
+            elif what == "I":
+                column_in(h, n, within)
+                settle(n, "q")
+            elif what == "P":
+                pass_on(h, n, within)
+            elif what == "X":
+                cross(h, n, within)
+                settle(n, "xy")
+            elif what == "D":
+                landed(pile(h, 2, flat(h, n, within)), got_diag.at[h, n])
+                settle(n, "d")
+            elif what == "U":
+                tall_out(h, n)
+            else:
+                spread_tall(h, n, within)
+                if not (within and n == 0):
+                    settle(n, "xyd")
 
     cents_in.wait()
     reduce_in(0, 0)
@@ -469,7 +455,12 @@
     for i in range(planes - 1, pieces_first):
         first_piece(i)
     renew(0)
-    start_inner(0)
+
+    @pl.when(inner)
+    def _():
+        own_start(0)
+        pass_on(0, 0, True)
+
     reduce_in(1, 0)
     pnorm = point_norms()
     mine[0] = (pnorm + low[0:1, :]) / width
@@ -478,23 +469,34 @@
     reduce_far(1, 0)
     reduce_in(1, 2)
     reduce_far(1, 1)
-    next_inner(0)
-    start_outer(0)
+
+    @pl.when(inner)
+    def _():
+        column_in(0, 1, True)
+        pass_on(0, 1, True)
+
     reduce_in(1, 3)
+
+    @pl.when(outer)
+    def _():
+        column_in(0, 0, False)
+        pass_on(0, 0, False)
+
     renew(1)
-    start_inner(1)
-    next_outer(0)
-    spread_cross(0, 0)
-    spread_cross(0, 1)
-    next_inner(1)
-    start_outer(1)
-    next_outer(1)
-    spread_cross(1, 0)
-    spread_cross(1, 1)
-    spread_diag(0, 0)
-    spread_diag(0, 1)
-    spread_diag(1, 0)
-    spread_diag(1, 1)
+
+    @pl.when(inner)
+    def _():
+        run(True, (
+            ("S", 1, 0), ("X", 0, 0), ("P", 1, 0), ("D", 0, 0), ("T", 0, 0), ("I", 1, 1), ("U", 0, 0), ("P", 1, 1),
+            ("X", 1, 0), ("X", 0, 1), ("T", 0, 1), ("D", 1, 0), ("D", 0, 1), ("X", 1, 1), ("D", 1, 1),
+        ))
+
+    @pl.when(outer)
+    def _():
+        run(False, (
+            ("I", 0, 1), ("P", 0, 1), ("X", 0, 0), ("I", 1, 0), ("P", 1, 0), ("X", 0, 1), ("I", 1, 1), ("P", 1, 1),
+            ("D", 0, 0), ("X", 1, 0), ("T", 0, 0), ("D", 0, 1), ("X", 1, 1), ("D", 1, 0), ("T", 0, 1), ("D", 1, 1),
+        ))
 
     mine[1] = (pnorm + low[1:2, :]) / width
     min_copies.append(ship(mine.at[1], theirs.at[1], sent_min.at[1], got_min.at[1], "cent", partner))
@@ -515,8 +517,8 @@
         for h in range(PARTS):
             sent_all(pile(h, 3 * PLANE, (share + flat(h, 1, True)) // 2), sent_gath.at[h])
             sent_all(pile(h, 6, share), sent_col.at[h])
-            if TALL[h]:
-                sent_all(pile(h, 9, 2 * TALL[h]), sent_tall.at[h])
+            if TALL[h][0]:
+                sent_all(pile(h, 6, TALL[h][0] + 2 * TALL[h][1]), sent_tall.at[h])
 
     for n, copy in enumerate(min_copies):
         copy.wait()
@@ -576,7 +578,7 @@
             dma((1,)), dma((PARTS, planes)), dma((1,)), dma((1,)),
             dma((1,)), dma((PARTS, planes, 2)), dma((1,)), dma((PARTS, 2, 2)),
             dma((PARTS,)), dma((PARTS,)), dma((PARTS,)),
-            dma((PARTS, 2, 2)), dma((PARTS, 2)), dma((PARTS, 2)), dma((PARTS, 2)),
+            dma((PARTS, 2, 2)), dma((PARTS, 2)), dma((PARTS, 2, 2)), dma((PARTS, 2)),
             dma((1,)), dma((2,)), dma((2,)),
         ],
         compiler_params=pltpu.CompilerParams(

time: 73.8 us -> 71.6 us (0.970)
  Pallas kernels: 72.9 us -> 70.6 us
    pallas_call x1, Pallas kernels: 70.8 us -> 68.5 us  [fused(): pl.pallas_call(functools.partial(lloyd_kernel, rows, cap, share), out_sha...]
where the time goes in v7:
time: 71.6 us; the launch traced here: 71.4 us
  Pallas kernels  70.6 us (99%)
  between operations  0.8 us (1%)
    pallas_call x1, Pallas kernels, fused(): pl.pallas_call(functools.partial(lloyd_kernel, rows, cap, share), out_sha...  68.5 us
    pallas_call x1, Pallas kernels, fused(): pl.pallas_call(deliver, out_shape=shapes, in_specs=[vmem, vmem], out_spec...  2.03 us

profile of v7, /device:TPU:0, one launch (start us, length us, event | category | flops | bytes accessed | tf_op | source)
XLA Modules:
  0.0 71.4 jit_solution(8408186073636584534)
XLA Ops:
  0.6 68.5 %shard_map.50 = (f32[2,1024]{1,0:T(2,128)S(1)}, bf16[16,128,1024]{2,1,0:T(8,128)(2,1)S(1)}) custom-call(s32[1,1024]{1,0:T(1,128)} %bitcast.2, bf16[1024,1024]{1,0:T(8,128)(2,1)} %points_hbm.1, bf16[2048,1024]{1,0:T(8,128)(2,1)} %cents_hbm.1), custom_call_target="tpu_custom_call" | custom-call | tf_op jit(solution)/shard_map/pallas_call | solution.py:551
  69.2 2.0 %shard_map.51 = (f32[2,1024]{1,0:T(2,128)}, bf16[16,128,1024]{2,1,0:T(8,128)(2,1)}) custom-call(f32[2,1024]{1,0:T(2,128)S(1)} %get-tuple-element.6.near_ref, bf16[16,128,1024]{2,1,0:T(8,128)(2,1)S(1)} %get-tuple-element.7.gath_ref), custom_call_target="tpu_custom_call" | custom-call | tf_op jit(solution)/shard_map/pallas_call | solution.py:592

commit v8 on v7

--- a/solution.py
+++ b/solution.py
@@ -359,11 +359,14 @@
             return share - TALL[h][0] * n
         return share - TALL[h][1]
 
+    def pass_block(h, n, p, within):
+        part = one(h, n, me, p, 0, flat(h, n, within))
+        for target in (xpeer, ypeer):
+            ship(part, part, sent_gath.at[h], got_side.at[h, n, p], "rows", target)
+
     def pass_on(h, n, within):
         for p in range(2):
-            part = one(h, n, me, p, 0, flat(h, n, within))
-            for target in (xpeer, ypeer):
-                ship(part, part, sent_gath.at[h], got_side.at[h, n, p], "rows", target)
+            pass_block(h, n, p, within)
 
     def own_start(h):
         for p in range(2):
@@ -377,6 +380,7 @@
             landed(part, got_col.at[h, n, p])
             if within:
                 ship(part, part, sent_col.at[h], got_col.at[h, n, p], "rows", beside)
+            pass_block(h, n, p, within)
 
     def cross(h, n, within):
         count = flat(h, n, within)
@@ -473,29 +477,27 @@
     @pl.when(inner)
     def _():
         column_in(0, 1, True)
-        pass_on(0, 1, True)
 
     reduce_in(1, 3)
 
     @pl.when(outer)
     def _():
         column_in(0, 0, False)
-        pass_on(0, 0, False)
 
     renew(1)
 
     @pl.when(inner)
     def _():
         run(True, (
-            ("S", 1, 0), ("X", 0, 0), ("P", 1, 0), ("D", 0, 0), ("T", 0, 0), ("I", 1, 1), ("U", 0, 0), ("P", 1, 1),
-            ("X", 1, 0), ("X", 0, 1), ("T", 0, 1), ("D", 1, 0), ("D", 0, 1), ("X", 1, 1), ("D", 1, 1),
+            ("S", 1, 0), ("X", 0, 0), ("P", 1, 0), ("D", 0, 0), ("T", 0, 0), ("I", 1, 1), ("U", 0, 0), ("X", 1, 0),
+            ("X", 0, 1), ("T", 0, 1), ("D", 1, 0), ("D", 0, 1), ("X", 1, 1), ("D", 1, 1),
         ))
 
     @pl.when(outer)
     def _():
         run(False, (
-            ("I", 0, 1), ("P", 0, 1), ("X", 0, 0), ("I", 1, 0), ("P", 1, 0), ("X", 0, 1), ("I", 1, 1), ("P", 1, 1),
-            ("D", 0, 0), ("X", 1, 0), ("T", 0, 0), ("D", 0, 1), ("X", 1, 1), ("D", 1, 0), ("T", 0, 1), ("D", 1, 1),
+            ("I", 0, 1), ("X", 0, 0), ("I", 1, 0), ("X", 0, 1), ("I", 1, 1), ("X", 1, 0), ("X", 1, 1), ("T", 0, 0),
+            ("D", 0, 0), ("D", 0, 1), ("T", 0, 1), ("D", 1, 0), ("D", 1, 1),
         ))
 
     mine[1] = (pnorm + low[1:2, :]) / width

time: 71.6 us -> 69.1 us (0.965)
  Pallas kernels: 70.6 us -> 68.1 us
    pallas_call x1, Pallas kernels: 68.5 us -> 66 us  [fused(): pl.pallas_call(functools.partial(lloyd_kernel, rows, cap, share), out_sha...]
where the time goes in v8:
time: 69.1 us; the launch traced here: 68.9 us
  Pallas kernels  68.1 us (99%)
  between operations  0.8 us (1%)
    pallas_call x1, Pallas kernels, fused(): pl.pallas_call(functools.partial(lloyd_kernel, rows, cap, share), out_sha...  66 us
    pallas_call x1, Pallas kernels, fused(): pl.pallas_call(deliver, out_shape=shapes, in_specs=[vmem, vmem], out_spec...  2.03 us

profile of v8, /device:TPU:0, one launch (start us, length us, event | category | flops | bytes accessed | tf_op | source)
XLA Modules:
  0.0 68.9 jit_solution(2679384514427947606)
XLA Ops:
  0.6 66.0 %shard_map.50 = (f32[2,1024]{1,0:T(2,128)S(1)}, bf16[16,128,1024]{2,1,0:T(8,128)(2,1)S(1)}) custom-call(s32[1,1024]{1,0:T(1,128)} %bitcast.2, bf16[1024,1024]{1,0:T(8,128)(2,1)} %points_hbm.1, bf16[2048,1024]{1,0:T(8,128)(2,1)} %cents_hbm.1), custom_call_target="tpu_custom_call" | custom-call | tf_op jit(solution)/shard_map/pallas_call | solution.py:553
  66.7 2.0 %shard_map.51 = (f32[2,1024]{1,0:T(2,128)}, bf16[16,128,1024]{2,1,0:T(8,128)(2,1)}) custom-call(f32[2,1024]{1,0:T(2,128)S(1)} %get-tuple-element.6.near_ref, bf16[16,128,1024]{2,1,0:T(8,128)(2,1)S(1)} %get-tuple-element.7.gath_ref), custom_call_target="tpu_custom_call" | custom-call | tf_op jit(solution)/shard_map/pallas_call | solution.py:594

commit v9 on v8

--- a/solution.py
+++ b/solution.py
@@ -489,7 +489,7 @@
     @pl.when(inner)
     def _():
         run(True, (
-            ("S", 1, 0), ("X", 0, 0), ("P", 1, 0), ("D", 0, 0), ("T", 0, 0), ("I", 1, 1), ("U", 0, 0), ("X", 1, 0),
+            ("S", 1, 0), ("X", 0, 0), ("P", 1, 0), ("D", 0, 0), ("T", 0, 0), ("I", 1, 1), ("X", 1, 0), ("U", 0, 0),
             ("X", 0, 1), ("T", 0, 1), ("D", 1, 0), ("D", 0, 1), ("X", 1, 1), ("D", 1, 1),
         ))
 

time: 69.1 us -> 69.1 us (level)
  no operation moved by 1% of the time
where the time goes in v9:
time: 69.1 us; the launch traced here: 68.9 us
  Pallas kernels  68.1 us (99%)
  between operations  0.8 us (1%)
    pallas_call x1, Pallas kernels, fused(): pl.pallas_call(functools.partial(lloyd_kernel, rows, cap, share), out_sha...  66 us
    pallas_call x1, Pallas kernels, fused(): pl.pallas_call(deliver, out_shape=shapes, in_specs=[vmem, vmem], out_spec...  2.03 us

profile of v9, /device:TPU:0, one launch (start us, length us, event | category | flops | bytes accessed | tf_op | source)
XLA Modules:
  0.0 68.9 jit_solution(8810465007129088096)
XLA Ops:
  0.6 66.0 %shard_map.50 = (f32[2,1024]{1,0:T(2,128)S(1)}, bf16[16,128,1024]{2,1,0:T(8,128)(2,1)S(1)}) custom-call(s32[1,1024]{1,0:T(1,128)} %bitcast.2, bf16[1024,1024]{1,0:T(8,128)(2,1)} %points_hbm.1, bf16[2048,1024]{1,0:T(8,128)(2,1)} %cents_hbm.1), custom_call_target="tpu_custom_call" | custom-call | tf_op jit(solution)/shard_map/pallas_call | solution.py:553
  66.7 2.0 %shard_map.51 = (f32[2,1024]{1,0:T(2,128)}, bf16[16,128,1024]{2,1,0:T(8,128)(2,1)}) custom-call(f32[2,1024]{1,0:T(2,128)S(1)} %get-tuple-element.6.near_ref, bf16[16,128,1024]{2,1,0:T(8,128)(2,1)S(1)} %get-tuple-element.7.gath_ref), custom_call_target="tpu_custom_call" | custom-call | tf_op jit(solution)/shard_map/pallas_call | solution.py:594
